TPU v7x, 128 devices: a whole 4x4x4 slice. The times are simulated.
128 devices in a mesh: band: 16 (over z_hi, x, core), ga: 8 (over y, z_lo).
Axes of the slice: x: 4, y: 4, z: 4 (z_hi: 2, z_lo: 2; z = z_hi * 2 + z_lo), core: 2. Of those that a mesh axis runs over, the one named last changes fastest.
Arguments:
- wave_coef: bfloat16 [8192, 32768], P('band', 'ga'), may hold values from -0.03125 to 0.03125
- projector: bfloat16 [64, 27, 32768], P('band', None, 'ga'), may hold values from -6 to 6
- occupation: float32 [8192], P('band'), may hold values from 0.25 to 4
- species: int32 [64], replicated, may hold values from 0 to 3
- layer_in: float32 [4, 729, 100], replicated, may hold values from -1.25 to 1.25
- bias_in: float32 [4, 100], replicated, may hold values from -3 to 3
- layer_out: float32 [4, 100], replicated, may hold values from -0.625 to 0.625
Outputs:
- corrected: bfloat16 [8192, 32768], P('band', 'ga')
All inputs are finite; a program needn't handle non-finite values.
Results may differ from a plain program's by a relative error of at most 0.0049.
Values may be sent and summed in bfloat16 or wider, within the bound.
A program may use at most 128 MiB of HBM per device.

v0:
```python
import jax
import jax.numpy as jnp
from jax import lax
from jax.sharding import PartitionSpec as P


def split_up(value, dim, count):
    before, after = (value.shape[:dim], value.shape[dim + 1 :])
    return jnp.moveaxis(value.reshape(*before, count, -1, *after), dim, 0)


def summed_on_arrival(value, axis, dim):
    pieces = split_up(value, dim, lax.axis_size(axis))
    arrived = lax.all_to_all(pieces, axis, split_axis=0, concat_axis=0, tiled=True)
    return arrived.sum(axis=0)


def from_everyone(value, axis):
    count = lax.axis_size(axis)
    return lax.all_to_all(
        jnp.broadcast_to(value[None], (count, *value.shape)), axis, 0, 0, tiled=True
    )


def taken_together(value, axis):
    everything = from_everyone(value, axis)
    return jnp.sum(everything, axis=0)


def in_order(pieces, dim):
    pieces = jnp.moveaxis(pieces, 0, dim)
    shape = pieces.shape
    return pieces.reshape(*shape[:dim], shape[dim] * shape[dim + 1], *shape[dim + 2 :])


def gathered_copies(value, axis, dim):
    pieces = from_everyone(value, axis)
    return in_order(pieces, dim)


def descriptor_step(density, kinds, layer_in, bias_in, layer_out, orbitals):
    atoms_here = density.shape[0]
    nspecies = layer_in.shape[0]
    onehot = (kinds[:, None] == jnp.arange(nspecies, dtype=jnp.int32)[None, :]).astype(jnp.float32)
    weight_atom = jnp.einsum("as,sfh->afh", onehot, layer_in, precision=lax.Precision.HIGHEST)
    bias_atom = jnp.dot(onehot, bias_in, precision=lax.Precision.HIGHEST)
    out_atom = jnp.dot(onehot, layer_out, precision=lax.Precision.HIGHEST)
    preact = (
        jnp.einsum(
            "af,afh->ah",
            density.reshape(atoms_here, orbitals * orbitals),
            weight_atom,
            precision=lax.Precision.HIGHEST,
        )
        + bias_atom
    )
    activation = jnp.tanh(preact)
    slopes = out_atom * (1.0 - activation * activation)
    gradient = jnp.einsum(
        "afh,ah->af", weight_atom, slopes, precision=lax.Precision.HIGHEST
    ).reshape(atoms_here, orbitals, orbitals)
    return gradient + jnp.swapaxes(gradient, 1, 2)


def project(wave_coef, segment):
    return jnp.einsum("ng,akg->nak", wave_coef, segment, preferred_element_type=jnp.float32)


def body(wave_coef, projector, occupation, species, layer_in, bias_in, layer_out):
    orbitals = projector.shape[1]
    atoms_all = projector.shape[0] * lax.axis_size("band")
    bands_all = wave_coef.shape[0] * lax.axis_size("band")
    whole_proj = lax.all_gather(projector, "band", axis=0, tiled=True)
    partial_value = project(wave_coef, whole_proj)
    coefficient = summed_on_arrival(partial_value, "ga", 1)
    owned = coefficient.shape[1]
    first_atom = lax.axis_index("ga") * owned
    local_density = jnp.einsum(
        "n,nak,nal->akl", occupation, coefficient, coefficient, precision=lax.Precision.HIGHEST
    )
    density = taken_together(local_density, "band") / bands_all
    kinds = lax.dynamic_slice_in_dim(species, first_atom, owned, 0)
    symmetric = descriptor_step(density, kinds, layer_in, bias_in, layer_out, orbitals)
    factor = 1.0 / jnp.sqrt(jnp.float32(atoms_all * orbitals))
    applied = (
        jnp.einsum("akl,nal->nak", symmetric, coefficient, precision=lax.Precision.HIGHEST) * factor
    ).astype(jnp.bfloat16)
    applied_all = gathered_copies(applied, "ga", 1)
    corrected = jnp.einsum(
        "nak,akg->ng", applied_all, whole_proj, preferred_element_type=jnp.float32
    )
    return corrected.astype(jnp.bfloat16)


def solution(mesh):
    in_specs = (P("band", "ga"), P("band", None, "ga"), P("band"), P(), P(), P(), P())
    out_specs = P("band", "ga")
    return jax.shard_map(body, mesh=mesh, in_specs=in_specs, out_specs=out_specs, check_vma=False)
```

profile of v0, /device:TPU:1, one launch (start us, length us, event | category | flops | bytes accessed | tf_op | source)
XLA Modules:
  0.0 290.4 jit_solution(5469321530558367447)
XLA Ops:
  6.5 2.7 copy.24
  9.3 0.0 all-gather.2.cloned.1.call-update
  9.3 113.9 %all-gather.2.cloned.1.call-done = bf16[64,27,4096]{2,1,0:T(8,128)(2,1)} async-done(((bf16[4,27,4096]{2,1,0:T(8,128)(2,1)}), bf16[64,27,4096]{2,1,0:T(8,128)(2,1)}) %all-gather.2.cloned.1.call-update) | async-done | bytes 14155792 | tf_op jit(solution)/shard_map/all_gather | solution.py:73
  123.2 15.8 %fusion.11 = f32[512,8,8,27]{0,2,1,3:T(8,128)S(1)} fusion(bf16[64,27,4096]{2,1,0:T(8,128)(2,1)} %all-gather.2.cloned.1.call-done, bf16[512,4096]{1,0:T(8,128)(2,1)} %param.7), kind=kOutput, calls=%fused_computation.11 | convolution fusion | flops 7247757312 | bytes 21889024 | tf_op jit(solution)/shard_map/ng,akg->nak/dot_general | solution.py:66
  139.0 2.2 copy.67
  141.2 4.6 %all-to-all-start = ((f32[8,512,8,27]{1,2,3,0:T(8,128)}), f32[8,512,8,27]{1,2,3,0:T(8,128)}, u32[]{:S(2)}, u32[]{:S(2)}) async-start(f32[8,512,8,27]{1,2,3,0:T(8,128)} %bitcast.44), calls=%async_computation | async-start | bytes 7077888 | tf_op jit(solution)/shard_map/all_to_all | solution.py:14
  145.8 0.1 dynamic_slice.3
  145.9 50.5 %all-to-all-done = f32[8,512,8,27]{1,2,3,0:T(8,128)} async-done(((f32[8,512,8,27]{1,2,3,0:T(8,128)}), f32[8,512,8,27]{1,2,3,0:T(8,128)}, u32[]{:S(2)}, u32[]{:S(2)}) %all-to-all-start) | async-done | bytes 3538976 | tf_op jit(solution)/shard_map/all_to_all | solution.py:14
  196.4 2.4 reduce_sum.18
  198.9 1.1 fusion.24
  200.0 0.1 copy.30
  200.1 0.1 broadcast_bitcast_fusion
  200.2 2.3 reshape.28
  202.4 4.7 %all-to-all-start.1 = ((f32[16,1,5832]{2,1,0:T(1,128)}), f32[16,1,5832]{2,1,0:T(1,128)S(1)}, u32[]{:S(2)}, u32[]{:S(2)}) async-start(f32[16,1,5832]{2,1,0:T(1,128)} %reshape.28), calls=%async_computation.1 | async-start | bytes 753664 | tf_op jit(solution)/shard_map/all_to_all | solution.py:20
  207.2 0.2 fusion.28
  207.4 3.0 %fusion.30 = f32[8,729,100]{1,0,2:T(8,128)} fusion(f32[4,729,100]{1,0,2:T(4,128)S(1)} %copy-done, s32[8]{0:T(128)S(1)} %dynamic_slice.3), kind=kOutput, calls=%fused_computation.33 | convolution fusion | flops 27993632 | bytes 3499232 | tf_op jit(solution)/shard_map/as,sfh->afh/dot_general | solution.py:45
  210.3 6.4 %all-to-all-done.1 = f32[16,1,5832]{2,1,0:T(1,128)S(1)} async-done(((f32[16,1,5832]{2,1,0:T(1,128)}), f32[16,1,5832]{2,1,0:T(1,128)S(1)}, u32[]{:S(2)}, u32[]{:S(2)}) %all-to-all-start.1) | async-done | bytes 373280 | tf_op jit(solution)/shard_map/all_to_all | solution.py:20
  216.7 0.6 broadcast.10
  217.3 2.4 reduce
  219.6 1.6 reshape.29
  221.3 0.1 bitcast_reduce_fusion
  221.5 0.1 reshape.27
  221.6 4.5 %fusion.9 = f32[8,1,100]{2,1,0:T(1,128)S(1)} fusion(f32[8,729,1]{1,2,0:T(1,128)S(1)} %reshape.27, f32[8,729,100]{1,0,2:T(8,128)} %fusion.30), kind=kOutput, calls=%fused_computation.9 | convolution fusion | flops 6998400 | bytes 2359328 | tf_op jit(solution)/shard_map/af,afh->ah/dot_general | solution.py:49
  226.1 0.2 fusion.23
  226.3 2.3 fusion.7
  228.6 0.1 reshape.17
  228.8 0.1 copy.32
  228.9 0.9 fusion.19
  229.8 0.1 copy.34
  230.0 0.1 broadcast_in_dim.5
  230.1 25.0 %all_to_all.15 = bf16[8,512,8,27]{1,2,3,0:T(8,128)(2,1)S(1)} all-to-all(bf16[8,512,8,27]{1,2,3,0:T(8,128)(2,1)S(1)} %broadcast_in_dim.5), channel_id=1, replica_groups=mesh['band'=16,'ga'=8] {'ga'}, dimensions={0} | all-to-all | bytes 3538944 | tf_op jit(solution)/shard_map/all_to_all | solution.py:20
  255.1 28.4 %bitcast_convert_fusion = bf16[512,4096]{1,0:T(8,128)(2,1)} fusion(bf16[64,27,4096]{2,1,0:T(8,128)(2,1)} %all-gather.2.cloned.1.call-done, bf16[8,512,8,27]{1,2,3,0:T(8,128)(2,1)S(1)} %all_to_all.15), kind=kOutput, calls=%fused_computation.4 | convolution fusion | flops 7249854464 | bytes 20119552 | tf_op jit(solution)/shard_map/nak,akg->ng/dot_general | solution.py:89
  (17 shorter events, 0.1 us)
Async XLA Ops:
  6.5 200.8 %copy-start = (f32[4,729,100]{1,0,2:T(4,128)S(1)}, f32[4,729,100]{1,0,2:T(4,128)}, u32[]{:S(2)}) copy-start(f32[4,729,100]{1,0,2:T(4,128)} %param.11) | copy-start | bytes 3499204
  6.5 116.7 %all-gather.2.cloned.1.call-start = ((), (), s32[]{:S(2)}) async-start(), calls=%async_computation.3 | async-start | bytes 17825792 | tf_op jit(solution)/shard_map/all_gather | solution.py:73
  141.2 4.6 %copy-start.5 = (s32[64]{0:T(128)S(1)}, s32[64]{0:T(128)}, u32[]{:S(2)}) copy-start(s32[64]{0:T(128)} %param.10) | copy-start | bytes 772
  141.2 55.2 %all-to-all-start = ((f32[8,512,8,27]{1,2,3,0:T(8,128)}), f32[8,512,8,27]{1,2,3,0:T(8,128)}, u32[]{:S(2)}, u32[]{:S(2)}) async-start(f32[8,512,8,27]{1,2,3,0:T(8,128)} %bitcast.44), calls=%async_computation | async-start | bytes 7077888 | tf_op jit(solution)/shard_map/all_to_all | solution.py:14
  145.8 53.0 %copy-start.2 = (f32[512]{0:T(512)S(1)}, f32[512]{0:T(512)}, u32[]{:S(2)}) copy-start(f32[512]{0:T(512)} %param.9) | copy-start | bytes 6148
  200.0 7.2 %copy-start.3 = (f32[4,100]{1,0:T(4,128)S(1)}, f32[4,100]{1,0:T(4,128)}, u32[]{:S(2)}) copy-start(f32[4,100]{1,0:T(4,128)} %param.13) | copy-start | bytes 4804
  202.4 14.2 %all-to-all-start.1 = ((f32[16,1,5832]{2,1,0:T(1,128)}), f32[16,1,5832]{2,1,0:T(1,128)S(1)}, u32[]{:S(2)}, u32[]{:S(2)}) async-start(f32[16,1,5832]{2,1,0:T(1,128)} %reshape.28), calls=%async_computation.1 | async-start | bytes 753664 | tf_op jit(solution)/shard_map/all_to_all | solution.py:20
  221.3 4.8 %copy-start.4 = (f32[4,100]{1,0:T(4,128)S(1)}, f32[4,100]{1,0:T(4,128)}, u32[]{:S(2)}) copy-start(f32[4,100]{1,0:T(4,128)} %param.12) | copy-start | bytes 4804
  221.6 4.7 %copy-start.1 = (f32[8,729,100]{1,0,2:T(8,128)S(1)}, f32[8,729,100]{1,0,2:T(8,128)}, u32[]{:S(2)}) copy-start(f32[8,729,100]{1,0,2:T(8,128)} %fusion.30) | copy-start | bytes 6998404
Sparse Core Ops, SparseCore 0:
  9.8 113.3 all-gather.1
where the time goes:
time: 292 us; the launch traced here: 290 us
  waiting for transfers between devices  171 us (59%)
  matrix products  56.3 us (19%)
  blocking collectives  25 us (9%)
  between operations  13.6 us (5%)
  local copies, waits for them, and re-layouts  10.4 us (4%)
  starting transfers between devices  9.34 us (3%)
  other arithmetic  4.98 us (2%)
    all_gather x1, waiting for transfers between devices, body(): whole_proj = lax.all_gather(projector, 'band', axis=0, tiled=True)  114 us
    all_to_all x1, waiting for transfers between devices, summed_on_arrival(): lax.all_to_all(pieces, axis, split_axis=0, concat_axis=0, tiled=True)  50.5 us
    dot_general x1, matrix products, body(): jnp.einsum('nak,akg->ng', applied_all, whole_proj, preferred_element_type...  28.4 us
    all_to_all x1, blocking collectives, from_everyone(): lax.all_to_all(jnp.broadcast_to(value[None], (count, *value.shape)), axis...  25 us
    dot_general x1, matrix products, project(): jnp.einsum('ng,akg->nak', wave_coef, segment, preferred_element_type=jnp....  15.8 us
    unnamed x16, local copies, waits for them, and re-layouts  6.79 us
    all_to_all x1, waiting for transfers between devices, from_everyone(): lax.all_to_all(jnp.broadcast_to(value[None], (count, *value.shape)), axis...  6.37 us
  transfers between devices with their start and end apart: 3, of which 3 were waited for; matrix products, arithmetic and copies ran while one was open for 1% of the time, Pallas kernels for 0%

commit v1 on v0

v1 whole, which is shorter than its diff:
```python
import functools
import math

import jax
import jax.numpy as jnp
from jax import lax
from jax.experimental import pallas as pl
from jax.experimental.pallas import tpu as pltpu
from jax.sharding import PartitionSpec as P

MESH = pl.DeviceIdType.MESH
F32 = jnp.float32
BF16 = jnp.bfloat16

K = 27
KP = 28
SLOT = 4 * KP
PAIR = 2 * SLOT
NZ = 80
HID = 100

ORDER = ((0, 0), (0, 3), (0, 1), (1, 0), (1, 3), (1, 1), (0, 2), (1, 2))

TREE = (
    ("z10", 0, NZ), ("x10", NZ, 32),
    ("z03", 0, NZ), ("x03", NZ, 32), ("z01", 0, NZ), ("x01", NZ, 32),
    ("x02a", NZ, 16), ("x02b", NZ + 16, 16), ("z02a", 0, 48), ("z02b", 48, 32),
    ("z13", 0, NZ), ("z11", 0, NZ), ("x13", NZ, 32), ("x11", NZ, 32),
    ("x12a", NZ, 16), ("x12b", NZ + 16, 16), ("z12a", 0, 32), ("z12b", 32, 48),
)
TREE_ID = {name: i for i, (name, _, _) in enumerate(TREE)}
NT = len(TREE)


def body_kernel(bands_all, w_hbm, p_hbm, occ_ref, species_ref, lin_hbm, bias_ref, lout_ref, out_ref,
                w, tab, part, part16, ry, zs, zr, cfull, lin, dsend, dpart, drecv, xs, xall, appt, app, bd,
                lsem, tss, tsr, d2s, d2r, rys, ryr, zss, zsr, ags, agr, dens_s, dens_r, xss, xsr):
    band = lax.axis_index("band")
    ga = lax.axis_index("ga")
    zh, x, c = band // 8, (band // 2) % 4, band % 2
    y, zl = ga // 2, ga % 2

    def at(dz=0, dx=0, dc=0, dy=0, dl=0):
        nzh, nx, nc = (zh + dz) % 2, (x + dx) % 4, (c + dc) % 2
        ny, nzl = (y + dy) % 4, (zl + dl) % 2
        return (nzh * 8 + nx * 2 + nc, ny * 2 + nzl)

    def slot_row(dz, dx, dc):
        nzh, nx, nc = (zh + dz) % 2, (x + dx) % 4, (c + dc) % 2
        return (nzh * 8 + nx * 2 + nc) * SLOT

    def pair_row(dz, dx):
        return (((zh + dz) % 2) * 4 + (x + dx) % 4) * PAIR

    def rows(ref, start, count):
        return ref.at[pl.ds(pl.multiple_of(start, 16), count)]

    wcopy = pltpu.make_async_copy(w_hbm, w, lsem.at[0])
    own_row = slot_row(0, 0, 0)
    pcopy = pltpu.make_async_copy(p_hbm, rows(tab, own_row, SLOT), lsem.at[1])
    lcopy = pltpu.make_async_copy(lin_hbm, lin, lsem.at[2])
    pcopy.start()
    wcopy.start()
    lcopy.start()

    barrier = pltpu.get_barrier_semaphore()
    partners = [at(dc=1)]
    for dz in range(2):
        for dx in range(4):
            if dz or dx:
                partners.append(at(dz=dz, dx=dx))
    for dy in range(4):
        for dl in range(2):
            if dy or dl:
                partners.append(at(dy=dy, dl=dl))
                partners.append(at(dy=dy, dl=dl, dc=1))
    for partner in partners:
        pl.semaphore_signal(barrier, inc=1, device_id=partner, device_id_type=MESH)
    pl.semaphore_wait(barrier, len(partners))
    pcopy.wait()

    sends = []

    def remote(src, dst, ss, rs, device):
        copy = pltpu.make_async_remote_copy(
            src_ref=src, dst_ref=dst, send_sem=ss, recv_sem=rs, device_id=device, device_id_type=MESH
        )
        copy.start()
        sends.append(copy)

    def arrived(dst, ss, rs):
        pltpu.make_async_remote_copy(
            src_ref=dst, dst_ref=dst, send_sem=ss, recv_sem=rs, device_id=at(dc=1), device_id_type=MESH
        ).wait_recv()

    def tree_send(name, dz, dx, device):
        i = TREE_ID[name]
        _, first, count = TREE[i]
        ref = rows(tab, slot_row(dz, dx, 0) + first, count)
        remote(ref, ref, tss.at[i], tsr.at[i], device)

    def tree_wait(name, dz, dx):
        i = TREE_ID[name]
        _, first, count = TREE[i]
        arrived(rows(tab, slot_row(dz, dx, 0) + first, count), tss.at[i], tsr.at[i])

    def across(i, dz, dx):
        ref = rows(tab, slot_row(dz, dx, 0), SLOT)
        remote(ref, ref, d2s.at[i], d2r.at[i], at(dc=1))

    def across_wait(i, dz, dx):
        arrived(rows(tab, slot_row(dz, dx, 1), SLOT), d2s.at[i], d2r.at[i])

    right, left, over = at(dx=1), at(dx=3), at(dz=1)

    def project(i):
        dz, dx = ORDER[i]
        base = pl.multiple_of(pair_row(dz, dx), 16)

        def half(t, carry):
            wt = w[pl.ds(pl.multiple_of(t * 256, 256), 256), :]
            got = lax.dot_general(
                tab[pl.ds(base, PAIR), :], wt, (((1,), (1,)), ((), ())), preferred_element_type=F32
            )
            cols = pl.ds(pl.multiple_of(t * 256, 256), 256)
            part[i, :, cols] = got
            part16[i, :, cols] = got.astype(BF16)
            return carry

        lax.fori_loop(0, 2, half, 0)
        for dy in range(1, 4):
            piece = pl.ds(pl.multiple_of(((y + dy) % 4) * 128, 128), 128)
            remote(part16.at[i, :, piece], ry.at[i, 3 - dy], rys.at[i, 3 - dy], ryr.at[i, 3 - dy], at(dy=dy))

    mine = pl.ds(pl.multiple_of(y * 128, 128), 128)

    def reduce_y(i):
        total = part[i, :, mine]
        for j in range(3):
            arrived(ry.at[i, j], rys.at[i, j], ryr.at[i, j])
        for j in range(3):
            total = total + ry[i, j].astype(F32)
        zs[i] = total.astype(BF16)
        remote(zs.at[i], zr.at[i], zss.at[i], zsr.at[i], at(dl=1))

    def reduce_z(i):
        dz, dx = ORDER[i]
        pair = pl.ds(pl.multiple_of(pair_row(dz, dx), 16), PAIR)
        arrived(zr.at[i], zss.at[i], zsr.at[i])
        cfull[pair, mine] = (zs[i].astype(F32) + zr[i].astype(F32)).astype(BF16)
        for dy in range(1, 4):
            ref = cfull.at[pair, mine]
            remote(ref, ref, ags.at[i, 3 - dy], agr.at[i, 3 - dy], at(dy=dy))

    def gathered(i):
        dz, dx = ORDER[i]
        pair = pl.ds(pl.multiple_of(pair_row(dz, dx), 16), PAIR)
        for dy in range(1, 4):
            piece = pl.ds(pl.multiple_of(((y + dy) % 4) * 128, 128), 128)
            arrived(cfull.at[pair, piece], ags.at[i, dy - 1], agr.at[i, dy - 1])

    tree_send("z10", 0, 0, over)
    tree_send("x03", 0, 0, right)
    tree_send("x01", 0, 0, left)
    across(0, 0, 0)
    tree_send("z03", 0, 0, right)
    tree_send("z01", 0, 0, left)
    tree_send("x10", 0, 0, over)

    wcopy.wait()
    across_wait(0, 0, 0)
    project(0)
    tree_wait("x03", 0, 3)
    tree_send("x02a", 0, 3, right)
    tree_send("x13", 0, 3, over)
    tree_wait("x01", 0, 1)
    tree_send("x02b", 0, 1, left)
    tree_send("x11", 0, 1, over)
    reduce_y(0)
    reduce_z(0)

    tree_wait("z10", 1, 0)
    tree_send("z13", 1, 0, right)
    tree_send("z11", 1, 0, left)
    tree_wait("z03", 0, 3)
    tree_send("z02a", 0, 3, right)
    across(1, 0, 3)
    tree_wait("z01", 0, 1)
    tree_send("z02b", 0, 1, left)
    across(2, 0, 1)
    tree_wait("x10", 1, 0)
    across(3, 1, 0)
    across_wait(1, 0, 3)
    project(1)
    tree_wait("x02a", 0, 2)
    tree_send("x12a", 0, 2, over)
    tree_wait("x02b", 0, 2)
    tree_send("x12b", 0, 2, over)
    across_wait(2, 0, 1)
    project(2)
    reduce_y(1)
    across_wait(3, 1, 0)
    project(3)
    reduce_z(1)
    reduce_y(2)
    reduce_y(3)
    reduce_z(2)
    reduce_z(3)

    tree_wait("z13", 1, 3)
    tree_send("z12a", 1, 3, right)
    tree_wait("z11", 1, 1)
    tree_send("z12b", 1, 1, left)
    tree_wait("x13", 1, 3)
    across(4, 1, 3)
    tree_wait("x11", 1, 1)
    across(5, 1, 1)
    across_wait(4, 1, 3)
    project(4)
    across_wait(5, 1, 1)
    project(5)
    reduce_y(4)
    reduce_y(5)

    tree_wait("z02a", 0, 2)
    tree_wait("z02b", 0, 2)
    across(6, 0, 2)
    reduce_z(4)
    reduce_z(5)
    across_wait(6, 0, 2)
    project(6)
    reduce_y(6)
    for name in ("x12a", "x12b", "z12a", "z12b"):
        tree_wait(name, 1, 2)
    across(7, 1, 2)
    reduce_z(6)
    across_wait(7, 1, 2)
    project(7)
    for i in range(7):
        gathered(i)
    reduce_y(7)
    reduce_z(7)
    gathered(7)

    lane_atom = lax.broadcasted_iota(jnp.int32, (KP, SLOT), 1) // KP
    occ = occ_ref[...]
    for h in range(2):
        coef = cfull[pl.ds(pl.multiple_of(ga * PAIR + h * SLOT, 16), SLOT), :]
        weighted = coef.astype(F32) * occ
        high = weighted.astype(BF16)
        low = (weighted - high.astype(F32)).astype(BF16)
        dims = (((1,), (1,)), ((), ()))
        gram = lax.dot_general(high, coef, dims, preferred_element_type=F32) + lax.dot_general(
            low, coef, dims, preferred_element_type=F32
        )
        bd[...] = gram
        packed = jnp.zeros((KP, SLOT), F32)
        for a in range(4):
            packed = packed + jnp.where(lane_atom == a, bd[a * KP:(a + 1) * KP, :], 0.0)
        dsend[h, 0:KP, 0:SLOT] = packed
    remote(dsend.at[1 - c], drecv.at[7], dens_s.at[7], dens_r.at[7], at(dc=1))
    arrived(drecv.at[7], dens_s.at[7], dens_r.at[7])
    dpart[...] = dsend[c] + drecv[7]
    for dz in range(2):
        for dx in range(4):
            if dz or dx:
                j = dz * 4 + (4 - dx) % 4 - 1
                remote(dpart, drecv.at[j], dens_s.at[j], dens_r.at[j], at(dz=dz, dx=dx))
    lcopy.wait()
    for j in range(7):
        arrived(drecv.at[j], dens_s.at[j], dens_r.at[j])
    density = dpart[...]
    for j in range(7):
        density = density + drecv[j]
    density = density * (1.0 / bands_all)

    lane = lax.broadcasted_iota(jnp.int32, (K, SLOT), 1)
    grad_t = jnp.zeros((K, SLOT), F32)
    slot = 2 * ga + c
    for a in range(4):
        kind = species_ref[4 * slot + a]
        acc = jnp.zeros((K, HID), F32)
        for k in range(K):
            acc = acc + density[0:K, a * KP + k:a * KP + k + 1] * lin[kind, k * K:(k + 1) * K, :]
        preact = jnp.sum(acc, axis=0, keepdims=True) + bias_ref[kind]
        act = jnp.tanh(preact)
        slope = lout_ref[kind] * (1.0 - act * act)
        for k in range(K):
            column = jnp.sum(lin[kind, k * K:(k + 1) * K, :] * slope, axis=1, keepdims=True)
            grad_t = jnp.where(lane == a * KP + k, column, grad_t)
    bd[...] = jnp.zeros((SLOT, SLOT), F32)
    lane_atom_k = lane // KP
    for a in range(4):
        bd[a * KP:a * KP + K, :] = jnp.where(lane_atom_k == a, grad_t, 0.0)
    both = bd[...] + bd[...].T
    bd[...] = both
    packed = jnp.zeros((KP, SLOT), F32)
    for a in range(4):
        packed = packed + bd[a * KP:(a + 1) * KP, :]
    xs[0:KP, 0:SLOT] = packed
    xall[slot] = xs[...]
    for dy in range(4):
        for dl in range(2):
            for dc in range(2):
                if dy or dl or dc:
                    j = (((4 - dy) % 4) * 2 + dl) * 2 + dc
                    remote(xs, xall.at[slot], xss.at[j], xsr.at[j], at(dy=dy, dl=dl, dc=dc))
    for dy in range(4):
        for dl in range(2):
            for dc in range(2):
                if dy or dl or dc:
                    j = (dy * 2 + dl) * 2 + dc
                    from_slot = 2 * (((y + dy) % 4) * 2 + (zl + dl) % 2) + (c + dc) % 2
                    arrived(xall.at[from_slot], xss.at[j], xsr.at[j])

    factor = 1.0 / math.sqrt(64 * K)
    rows4 = lax.broadcasted_iota(jnp.int32, (SLOT, SLOT), 0) // KP
    lanes4 = lax.broadcasted_iota(jnp.int32, (SLOT, SLOT), 1) // KP
    same = rows4 == lanes4

    def apply(j, carry):
        packed = xall[j, 0:KP, 0:SLOT]
        for a in range(4):
            bd[a * KP:(a + 1) * KP, :] = packed
        full = jnp.where(same, bd[...], 0.0)
        high = full.astype(BF16)
        low = (full - high.astype(F32)).astype(BF16)
        at_rows = pl.ds(pl.multiple_of(j * SLOT, 16), SLOT)
        coef = cfull[at_rows, :]
        got = jnp.dot(high, coef, preferred_element_type=F32) + jnp.dot(low, coef, preferred_element_type=F32)
        appt[at_rows, :] = (got * factor).astype(BF16)
        return carry

    lax.fori_loop(0, 16, apply, 0)

    def turn(j, carry):
        block = pl.ds(pl.multiple_of(j * 256, 256), 256)
        app[:, block] = appt[block, :].T
        return carry

    lax.fori_loop(0, 7, turn, 0)

    def correct(t, carry):
        cols = pl.ds(pl.multiple_of(t * 512, 512), 512)
        out_ref[:, cols] = jnp.dot(app[...], tab[:, cols], preferred_element_type=F32).astype(BF16)
        return carry

    lax.fori_loop(0, 8, correct, 0)
    for copy in sends:
        copy.wait_send()


def body(wave_coef, projector, occupation, species, layer_in, bias_in, layer_out):
    atoms_here, orbitals, gs = projector.shape
    bands = wave_coef.shape[0]
    bands_all = bands * lax.axis_size("band")
    assert atoms_here == 4 and orbitals == K and bands == 512
    packed = jnp.pad(projector, ((0, 0), (0, KP - K), (0, 0))).reshape(SLOT, gs)
    any_space = pl.BlockSpec(memory_space=pl.ANY)
    vmem = pl.BlockSpec(memory_space=pltpu.VMEM)
    smem = pl.BlockSpec(memory_space=pltpu.SMEM)
    dma = pltpu.SemaphoreType.DMA
    return pl.pallas_call(
        functools.partial(body_kernel, bands_all),
        out_shape=jax.ShapeDtypeStruct((bands, gs), BF16),
        in_specs=[any_space, any_space, vmem, smem, any_space, vmem, vmem],
        out_specs=vmem,
        scratch_shapes=[
            pltpu.VMEM((bands, gs), BF16),
            pltpu.VMEM((16 * SLOT, gs), BF16),
            pltpu.VMEM((8, PAIR, bands), F32),
            pltpu.VMEM((8, PAIR, bands), BF16),
            pltpu.VMEM((8, 3, PAIR, 128), BF16),
            pltpu.VMEM((8, PAIR, 128), BF16),
            pltpu.VMEM((8, PAIR, 128), BF16),
            pltpu.VMEM((16 * SLOT, bands), BF16),
            pltpu.VMEM(layer_in.shape, F32),
            pltpu.VMEM((2, 32, 128), F32),
            pltpu.VMEM((32, 128), F32),
            pltpu.VMEM((8, 32, 128), F32),
            pltpu.VMEM((32, 128), F32),
            pltpu.VMEM((16, 32, 128), F32),
            pltpu.VMEM((16 * SLOT, bands), BF16),
            pltpu.VMEM((bands, 16 * SLOT), BF16),
            pltpu.VMEM((SLOT, SLOT), F32),
            dma((3,)), dma((NT,)), dma((NT,)), dma((8,)), dma((8,)),
            dma((8, 3)), dma((8, 3)), dma((8,)), dma((8,)), dma((8, 3)), dma((8, 3)),
            dma((8,)), dma((8,)), dma((16,)), dma((16,)),
        ],
        compiler_params=pltpu.CompilerParams(
            collective_id=0, has_side_effects=True, vmem_limit_bytes=62 * 2**20
        ),
        name="step",
    )(wave_coef, packed, occupation.reshape(1, bands), species, layer_in,
      bias_in.reshape(-1, 1, HID), layer_out.reshape(-1, 1, HID))


def solution(mesh):
    in_specs = (P("band", "ga"), P("band", None, "ga"), P("band"), P(), P(), P(), P())
    out_specs = P("band", "ga")
    return jax.shard_map(body, mesh=mesh, in_specs=in_specs, out_specs=out_specs, check_vma=False)
```

time: 292 us -> 142 us (0.49)
  waiting for transfers between devices: 171 us -> 0 us
  Pallas kernels: 0 us -> 133 us
  matrix products: 56.3 us -> 0 us
  blocking collectives: 25 us -> 0 us
  between operations: 13.6 us -> 0.03 us
  starting transfers between devices: 9.34 us -> 0 us
  other arithmetic: 4.98 us -> 0 us
    pallas_call x0 -> x1, Pallas kernels: none -> 133 us  [body(): pl.pallas_call(functools.partial(body_kernel, bands_all), out_shape=jax.S...]
    all_gather x1 -> x0, waiting for transfers between devices: 114 us -> none  [body(): whole_proj = lax.all_gather(projector, 'band', axis=0, tiled=True)]
    all_to_all x2 -> x0, waiting for transfers between devices: 56.9 us -> none  [the longest x1 50.5 us: summed_on_arrival(): lax.all_to_all(pieces, axis, split_axis=0, concat_axis=0, tiled=True)]
    dot_general x9 -> x0, matrix products: 56.3 us -> none  [the longest x1 28.4 us: body(): jnp.einsum('nak,akg->ng', applied_all, whole_proj, preferred_element_type...]
    all_to_all x1 -> x0, blocking collectives: 25 us -> none  [from_everyone(): lax.all_to_all(jnp.broadcast_to(value[None], (count, *value.shape)), axis...]
    all_to_all x2 -> x0, starting transfers between devices: 9.34 us -> none  [the longest x1 4.72 us: from_everyone(): lax.all_to_all(jnp.broadcast_to(value[None], (count, *value.shape)), axis...]
    unnamed x16 -> x5, local copies, waits for them, and re-layouts: 6.79 us -> 8.05 us
  transfers between devices with their start and end apart: 3 -> 0, of which waited for: 3 -> 0; matrix products, arithmetic and copies ran while one was open for 1% -> 0% of each run, Pallas kernels for 0% -> 0%
where the time goes in v1:
time: 142 us
  Pallas kernels  133 us (94%)
  local copies, waits for them, and re-layouts  9.27 us (7%)
    pallas_call x1, Pallas kernels, body(): pl.pallas_call(functools.partial(body_kernel, bands_all), out_shape=jax.S...  133 us
    unnamed x5, local copies, waits for them, and re-layouts  8.05 us

profile of v1, /device:TPU:1, one launch (start us, length us, event | category | flops | bytes accessed | tf_op | source)
XLA Modules:
  0.0 142.3 jit_solution(11475388335505523222)
XLA Ops:
  0.0 0.0 copy-start
  0.0 1.8 %copy.12 = bf16[4,27,4096]{2,1,0:T(8,128)(2,1)S(1)} copy(bf16[4,27,4096]{2,0,1:T(4,128)(2,1)} %param.8) | data formatting | bytes 1769472
  1.8 0.1 pad.4.clone
  1.9 1.1 reshape.12.p_hbm
  3.0 0.0 copy-done
  3.0 1.6 %copy.11.lin_hbm = f32[4,729,100]{2,1,0:T(8,128)} copy(f32[4,729,100]{1,0,2:T(4,128)S(1)} %copy-done) | data formatting | bytes 2332800 | tf_op args[4]
  4.6 133.0 %step.1 = bf16[512,4096]{1,0:T(8,128)(2,1)} custom-call(bf16[512,4096]{1,0:T(8,128)(2,1)} %w_hbm.1, bf16[112,4096]{1,0:T(8,128)(2,1)} %reshape.12.p_hbm, f32[1,512]{1,0:T(1,128)} %bitcast.3, s32[64]{0:T(128)} %species_ref.1, f32[4,729,100]{2,1,0:T(8,128)} %copy.11.lin_hbm, f32[4,1,100]{2,1,0:T(1,128)} %bitcast.4, f32[4,1,100]{2,1,0:T(1,128)} %bitcast.5), custom_call_target="tpu_custom_call" | custom-call | tf_op jit(solution)/shard_map/step/pallas_call | solution.py:363
  137.6 4.7 %copy.14 = bf16[512,4096]{1,0:T(8,128)(2,1)} copy(bf16[512,4096]{1,0:T(8,128)(2,1)} %step.1) | data formatting | bytes 8388608
Async XLA Ops:
  0.0 3.0 %copy-start = (f32[4,729,100]{1,0,2:T(4,128)S(1)}, f32[4,729,100]{1,0,2:T(4,128)}, u32[]{:S(2)}) copy-start(f32[4,729,100]{1,0,2:T(4,128)} %param.11) | copy-start | bytes 3499204

commit v2 on v1

v2 whole, which is shorter than its diff:
```python
import functools
import math

import jax
import jax.numpy as jnp
from jax import lax
from jax.experimental import pallas as pl
from jax.experimental.pallas import tpu as pltpu
from jax.sharding import PartitionSpec as P

MESH = pl.DeviceIdType.MESH
F32 = jnp.float32
BF16 = jnp.bfloat16

K = 27
KP = 28
SLOT = 4 * KP
PAIR = 2 * SLOT
HID = 100
SPECIES = 4

ORDER = ((0, 0), (0, 3), (0, 1), (1, 0), (1, 3), (1, 1), (0, 2), (1, 2))

PIECES = tuple((i, 0, PAIR) for i in range(7)) + ((7, 0, 80), (7, 144, 80), (7, 80, 64))

TREE = (
    ("z10", 32, 80), ("x10", 0, 32),
    ("z03", 32, 80), ("x03", 0, 32), ("z01", 32, 80), ("x01", 0, 32),
    ("x02a", 0, 16), ("x02b", 16, 16), ("z02a", 32, 48), ("z02b", 80, 32),
    ("z13", 32, 80), ("z11", 32, 80), ("x13", 0, 32), ("x11", 0, 32),
    ("x12a", 0, 16), ("x12b", 16, 16), ("z12a", 64, 16), ("z12b", 32, 32),
    ("z12c", 80, 16), ("z12d", 96, 16),
)
TREE_ID = {name: i for i, (name, _, _) in enumerate(TREE)}
NT = len(TREE)


def body_kernel(bands_all, w_hbm, p_hbm, occ_ref, species_ref, lin_hbm, bias_ref, lout_ref, app_out,
                tab_out, w, tab, pin, lraw, part, part16, ry, zs, zr, cfull, lin, dsend, dpart, drecv, xs, xall, appt, app, bd, bds,
                lsem, tabs, apps, tss, tsr, d2s, d2r, rys, ryr, zss, zsr, ags, agr, dens_s, dens_r, xss, xsr):
    band = lax.axis_index("band")
    ga = lax.axis_index("ga")
    zh, x, c = band // 8, (band // 2) % 4, band % 2
    y, zl = ga // 2, ga % 2

    def at(dz=0, dx=0, dc=0, dy=0, dl=0):
        nzh, nx, nc = (zh + dz) % 2, (x + dx) % 4, (c + dc) % 2
        ny, nzl = (y + dy) % 4, (zl + dl) % 2
        return (nzh * 8 + nx * 2 + nc, ny * 2 + nzl)

    def slot_row(dz, dx, dc):
        nzh, nx, nc = (zh + dz) % 2, (x + dx) % 4, (c + dc) % 2
        return (nzh * 8 + nx * 2 + nc) * SLOT

    def pair_row(dz, dx):
        return (((zh + dz) % 2) * 4 + (x + dx) % 4) * PAIR

    def row_in_slot(first, count, dc=0):
        return jnp.where((c + dc) % 2 == 0, first, SLOT - first - count)

    def rows(ref, start, count):
        return ref.at[pl.ds(pl.multiple_of(start, 16), count)]

    wcopy = pltpu.make_async_copy(w_hbm, w, lsem.at[0])
    own_row = slot_row(0, 0, 0)
    pcopy = pltpu.make_async_copy(p_hbm, pin, lsem.at[1])
    lcopy = pltpu.make_async_copy(lin_hbm, lraw, lsem.at[2])
    pcopy.start()
    wcopy.start()
    lcopy.start()

    barrier = pltpu.get_barrier_semaphore()
    partners = [at(dc=1)]
    for dz in range(2):
        for dx in range(4):
            if dz or dx:
                partners.append(at(dz=dz, dx=dx))
    for dy in range(4):
        for dl in range(2):
            if dy or dl:
                partners.append(at(dy=dy, dl=dl))
                partners.append(at(dy=dy, dl=dl, dc=1))
    for partner in partners:
        pl.semaphore_signal(barrier, inc=1, device_id=partner, device_id_type=MESH)
    pcopy.wait()

    def pack(t, carry):
        cols = pl.ds(pl.multiple_of(t * 512, 512), 512)
        flat = pin[:, :, cols].astype(F32).reshape(4 * K, 512)
        full = jnp.concatenate([flat, jnp.zeros((SLOT - 4 * K, 512), F32)], axis=0)
        tab[pl.ds(pl.multiple_of(own_row, 16), SLOT), cols] = full.astype(BF16)
        return carry

    lax.fori_loop(0, 8, pack, 0)
    pl.semaphore_wait(barrier, len(partners))

    sends = []

    def remote(src, dst, ss, rs, device):
        copy = pltpu.make_async_remote_copy(
            src_ref=src, dst_ref=dst, send_sem=ss, recv_sem=rs, device_id=device, device_id_type=MESH
        )
        copy.start()
        sends.append(copy)

    def arrived(dst, ss, rs):
        pltpu.make_async_remote_copy(
            src_ref=dst, dst_ref=dst, send_sem=ss, recv_sem=rs, device_id=at(dc=1), device_id_type=MESH
        ).wait_recv()

    def tree_send(name, dz, dx, device):
        i = TREE_ID[name]
        _, first, count = TREE[i]
        ref = rows(tab, slot_row(dz, dx, 0) + row_in_slot(first, count), count)
        remote(ref, ref, tss.at[i], tsr.at[i], device)

    def tree_wait(name, dz, dx):
        i = TREE_ID[name]
        _, first, count = TREE[i]
        arrived(rows(tab, slot_row(dz, dx, 0) + row_in_slot(first, count), count), tss.at[i], tsr.at[i])

    def across(i, dz, dx, first=0, count=SLOT):
        ref = rows(tab, slot_row(dz, dx, 0) + row_in_slot(first, count), count)
        remote(ref, ref, d2s.at[i], d2r.at[i], at(dc=1))

    def across_wait(i, dz, dx, first=0, count=SLOT):
        arrived(rows(tab, slot_row(dz, dx, 1) + row_in_slot(first, count, 1), count), d2s.at[i], d2r.at[i])

    flushes = []

    def flush(i):
        ref = rows(tab, pair_row(*ORDER[i]), PAIR)
        copy = pltpu.make_async_copy(ref, rows(tab_out, pair_row(*ORDER[i]), PAIR), tabs.at[i])
        copy.start()
        flushes.append(copy)

    right, left, over = at(dx=1), at(dx=3), at(dz=1)

    def project(*pieces):
        i = PIECES[pieces[0]][0]
        base = pair_row(*ORDER[i])

        def half(t, carry):
            cols = pl.ds(pl.multiple_of(t * 256, 256), 256)
            table = [tab[pl.ds(pl.multiple_of(base + PIECES[s][1], 16), PIECES[s][2]), :] for s in pieces]
            table = table[0] if len(pieces) == 1 else jnp.concatenate(table, axis=0)
            got = lax.dot_general(table, w[cols, :], (((1,), (1,)), ((), ())), preferred_element_type=F32)
            done = 0
            for s in pieces:
                _, first, count = PIECES[s]
                part[i, first:first + count, cols] = got[done:done + count]
                part16[i, first:first + count, cols] = got[done:done + count].astype(BF16)
                done += count
            return carry

        lax.fori_loop(0, 2, half, 0)
        for s in pieces:
            here = pl.ds(PIECES[s][1], PIECES[s][2])
            for dy in (2, 1, 3):
                lanes = pl.ds(pl.multiple_of(((y + dy) % 4) * 128, 128), 128)
                remote(part16.at[i, here, lanes], ry.at[i, 3 - dy, here], rys.at[s, 3 - dy], ryr.at[s, 3 - dy], at(dy=dy))

    mine = pl.ds(pl.multiple_of(y * 128, 128), 128)

    def reduce_y(s):
        i, first, count = PIECES[s]
        here = pl.ds(first, count)
        for j in range(3):
            arrived(ry.at[i, j, here], rys.at[s, j], ryr.at[s, j])
        total = part[i, here, mine]
        for j in range(3):
            total = total + ry[i, j, here].astype(F32)
        part[i, here, mine] = total
        zs[i, here] = total.astype(BF16)
        remote(zs.at[i, here], zr.at[i, here], zss.at[s], zsr.at[s], at(dl=1))

    def in_full(s):
        i, first, count = PIECES[s]
        return pl.ds(pl.multiple_of(pair_row(*ORDER[i]) + first, 16), count)

    def reduce_z(s):
        i, first, count = PIECES[s]
        here = pl.ds(first, count)
        arrived(zr.at[i, here], zss.at[s], zsr.at[s])
        cfull[in_full(s), mine] = (part[i, here, mine] + zr[i, here].astype(F32)).astype(BF16)
        for dy in (2, 1, 3):
            ref = cfull.at[in_full(s), mine]
            remote(ref, ref, ags.at[s, 3 - dy], agr.at[s, 3 - dy], at(dy=dy))

    def gathered(s):
        for dy in range(1, 4):
            lanes = pl.ds(pl.multiple_of(((y + dy) % 4) * 128, 128), 128)
            arrived(cfull.at[in_full(s), lanes], ags.at[s, dy - 1], agr.at[s, dy - 1])

    tree_send("z10", 0, 0, over)
    tree_send("x03", 0, 0, right)
    tree_send("x01", 0, 0, left)
    across(0, 0, 0)
    tree_send("z03", 0, 0, right)
    tree_send("z01", 0, 0, left)
    tree_send("x10", 0, 0, over)

    wcopy.wait()
    across_wait(0, 0, 0)
    project(0)
    flush(0)
    tree_wait("x03", 0, 3)
    tree_send("x02a", 0, 3, right)
    tree_send("x13", 0, 3, over)
    tree_wait("x01", 0, 1)
    tree_send("x02b", 0, 1, left)
    tree_send("x11", 0, 1, over)
    reduce_y(0)

    lcopy.wait()
    for kind in range(SPECIES):
        lin[kind] = lraw[:, kind, :].T

    tree_wait("z10", 1, 0)
    tree_send("z13", 1, 0, right)
    tree_send("z11", 1, 0, left)
    tree_wait("z03", 0, 3)
    tree_send("z02a", 0, 3, right)
    across(1, 0, 3)
    tree_wait("z01", 0, 1)
    tree_send("z02b", 0, 1, left)
    across(2, 0, 1)
    tree_wait("x10", 1, 0)
    across(3, 1, 0)
    tree_wait("x02a", 0, 2)
    tree_send("x12a", 0, 2, over)
    tree_wait("x02b", 0, 2)
    tree_send("x12b", 0, 2, over)
    across_wait(1, 0, 3)
    project(1)
    across_wait(2, 0, 1)
    project(2)
    across_wait(3, 1, 0)
    project(3)
    for i in (1, 2, 3):
        flush(i)
    reduce_z(0)
    reduce_y(1)
    reduce_y(2)
    reduce_y(3)

    tree_wait("z13", 1, 3)
    tree_send("z12a", 1, 3, right)
    tree_send("z12c", 1, 3, right)
    tree_wait("z11", 1, 1)
    tree_send("z12b", 1, 1, left)
    tree_send("z12d", 1, 1, left)
    tree_wait("x13", 1, 3)
    across(4, 1, 3)
    tree_wait("x11", 1, 1)
    across(5, 1, 1)
    reduce_z(1)
    across_wait(4, 1, 3)
    project(4)
    across_wait(5, 1, 1)
    project(5)
    flush(4)
    flush(5)
    reduce_z(2)
    reduce_z(3)
    reduce_y(4)

    tree_wait("z02a", 0, 2)
    tree_wait("z02b", 0, 2)
    across(6, 0, 2)
    reduce_y(5)
    across_wait(6, 0, 2)
    project(6)
    flush(6)
    reduce_z(4)
    reduce_z(5)
    tree_wait("x12a", 1, 2)
    tree_wait("x12b", 1, 2)
    tree_wait("z12a", 1, 2)
    tree_wait("z12b", 1, 2)
    across(7, 1, 2, 0, 80)
    across_wait(7, 1, 2, 0, 80)
    project(7, 8)
    tree_wait("z12c", 1, 2)
    tree_wait("z12d", 1, 2)
    across(8, 1, 2, 80, 32)
    across_wait(8, 1, 2, 80, 32)
    project(9)
    flush(7)
    reduce_y(6)
    reduce_y(7)
    reduce_y(8)
    reduce_y(9)
    reduce_z(6)
    reduce_z(7)
    reduce_z(8)
    reduce_z(9)
    for s in range(10):
        gathered(s)

    lane_atom = lax.broadcasted_iota(jnp.int32, (KP, SLOT), 1) % 4
    occ = occ_ref[...]
    for h in range(2):
        coef = cfull[pl.ds(pl.multiple_of(ga * PAIR + h * SLOT, 16), SLOT), :]
        weighted = coef.astype(F32) * occ
        high = weighted.astype(BF16)
        low = (weighted - high.astype(F32)).astype(BF16)
        dims = (((1,), (1,)), ((), ()))
        gram = lax.dot_general(high, coef, dims, preferred_element_type=F32) + lax.dot_general(
            low, coef, dims, preferred_element_type=F32
        )
        bd[:, 0:SLOT] = gram
        packed = jnp.zeros((KP, SLOT), F32)
        for a in range(4):
            packed = packed + jnp.where(lane_atom == a, bd[pl.ds(a, KP, stride=4), :][:, 0:SLOT], 0.0)
        dsend[h, 0:KP, 0:SLOT] = packed
    remote(dsend.at[1 - c], drecv.at[7], dens_s.at[7], dens_r.at[7], at(dc=1))
    arrived(drecv.at[7], dens_s.at[7], dens_r.at[7])
    dpart[...] = dsend[c] + drecv[7]
    for dz in range(2):
        for dx in range(4):
            if dz or dx:
                j = dz * 4 + (4 - dx) % 4 - 1
                remote(dpart, drecv.at[j], dens_s.at[j], dens_r.at[j], at(dz=dz, dx=dx))
    for j in range(7):
        arrived(drecv.at[j], dens_s.at[j], dens_r.at[j])
    density = dpart[...]
    for j in range(7):
        density = density + drecv[j]
    density = density * (1.0 / bands_all)

    lane = lax.broadcasted_iota(jnp.int32, (K, SLOT), 1)
    grad_t = jnp.zeros((K, SLOT), F32)
    slot = 2 * ga + c
    for a in range(4):
        kind = species_ref[4 * slot + a]
        acc = jnp.zeros((K, HID), F32)
        for k in range(K):
            acc = acc + density[0:K, 4 * k + a:4 * k + a + 1] * lin[kind, k * K:(k + 1) * K, :]
        preact = jnp.sum(acc, axis=0, keepdims=True) + bias_ref[kind]
        act = jnp.tanh(preact)
        slope = lout_ref[kind] * (1.0 - act * act)
        for k in range(K):
            column = jnp.sum(lin[kind, k * K:(k + 1) * K, :] * slope, axis=1, keepdims=True)
            grad_t = jnp.where(lane == 4 * k + a, column, grad_t)
    bd[...] = jnp.zeros((SLOT, 128), F32)
    pad = jnp.zeros((K, 128 - SLOT), F32)
    for a in range(4):
        bd[pl.ds(a, K, stride=4), :] = jnp.concatenate([jnp.where(lane % 4 == a, grad_t, 0.0), pad], axis=1)
    square = bd[:, 0:SLOT]
    bd[:, 0:SLOT] = square + square.T
    packed = jnp.zeros((KP, 128), F32)
    for a in range(4):
        packed = packed + bd[pl.ds(a, KP, stride=4), :]
    xs[0:KP, :] = packed
    xall[slot] = xs[...]
    for dy in range(4):
        for dl in range(2):
            for dc in range(2):
                if dy or dl or dc:
                    j = (((4 - dy) % 4) * 2 + dl) * 2 + dc
                    remote(xs, xall.at[slot], xss.at[j], xsr.at[j], at(dy=dy, dl=dl, dc=dc))
    for dy in range(4):
        for dl in range(2):
            for dc in range(2):
                if dy or dl or dc:
                    j = (dy * 2 + dl) * 2 + dc
                    from_slot = 2 * (((y + dy) % 4) * 2 + (zl + dl) % 2) + (c + dc) % 2
                    arrived(xall.at[from_slot], xss.at[j], xsr.at[j])

    factor = 1.0 / math.sqrt(64 * K)
    rows4 = lax.broadcasted_iota(jnp.int32, (SLOT, SLOT), 0) % 4
    lanes4 = lax.broadcasted_iota(jnp.int32, (SLOT, SLOT), 1) % 4
    same = rows4 == lanes4

    def apply(j, carry):
        for a in range(4):
            bds[j, pl.ds(a, KP, stride=4), :] = xall[j, 0:KP, :]
        full = jnp.where(same, bds[j, :, 0:SLOT], 0.0)
        high = full.astype(BF16)
        low = (full - high.astype(F32)).astype(BF16)
        at_rows = pl.ds(pl.multiple_of(j * SLOT, 16), SLOT)
        coef = cfull[at_rows, :]
        got = jnp.dot(high, coef, preferred_element_type=F32) + jnp.dot(low, coef, preferred_element_type=F32)
        appt[at_rows, :] = (got * factor).astype(BF16)
        return carry

    lax.fori_loop(0, 16, apply, 0, unroll=4)

    def turn(j, carry):
        block = pl.ds(pl.multiple_of(j * 256, 256), 256)
        app[:, block] = appt[block, :].T
        return carry

    lax.fori_loop(0, 7, turn, 0)
    last = pltpu.make_async_copy(app, app_out, apps)
    last.start()
    last.wait()
    for copy in flushes:
        copy.wait()
    for copy in sends:
        copy.wait_send()


def correct_kernel(app_ref, tab_ref, out_ref):
    out_ref[...] = jnp.dot(app_ref[...], tab_ref[...], preferred_element_type=F32).astype(BF16)


def body(wave_coef, projector, occupation, species, layer_in, bias_in, layer_out):
    atoms_here, orbitals, gs = projector.shape
    bands = wave_coef.shape[0]
    bands_all = bands * lax.axis_size("band")
    assert atoms_here == 4 and orbitals == K and bands == 512
    any_space = pl.BlockSpec(memory_space=pl.ANY)
    vmem = pl.BlockSpec(memory_space=pltpu.VMEM)
    smem = pl.BlockSpec(memory_space=pltpu.SMEM)
    dma = pltpu.SemaphoreType.DMA
    applied, table = pl.pallas_call(
        functools.partial(body_kernel, bands_all),
        out_shape=[jax.ShapeDtypeStruct((bands, 16 * SLOT), BF16), jax.ShapeDtypeStruct((16 * SLOT, gs), BF16)],
        in_specs=[any_space, any_space, vmem, smem, any_space, vmem, vmem],
        out_specs=[any_space, any_space],
        scratch_shapes=[
            pltpu.VMEM((bands, gs), BF16),
            pltpu.VMEM((16 * SLOT, gs), BF16),
            pltpu.VMEM((K, 4, gs), BF16),
            pltpu.VMEM((HID, SPECIES, K * K), F32),
            pltpu.VMEM((8, PAIR, bands), F32),
            pltpu.VMEM((8, PAIR, bands), BF16),
            pltpu.VMEM((8, 3, PAIR, 128), BF16),
            pltpu.VMEM((8, PAIR, 128), BF16),
            pltpu.VMEM((8, PAIR, 128), BF16),
            pltpu.VMEM((16 * SLOT, bands), BF16),
            pltpu.VMEM((SPECIES, K * K, HID), F32),
            pltpu.VMEM((2, 32, 128), F32),
            pltpu.VMEM((32, 128), F32),
            pltpu.VMEM((8, 32, 128), F32),
            pltpu.VMEM((32, 128), F32),
            pltpu.VMEM((16, 32, 128), F32),
            pltpu.VMEM((16 * SLOT, bands), BF16),
            pltpu.VMEM((bands, 16 * SLOT), BF16),
            pltpu.VMEM((SLOT, 128), F32),
            pltpu.VMEM((16, SLOT, 128), F32),
            dma((3,)), dma((8,)), dma, dma((NT,)), dma((NT,)), dma((9,)), dma((9,)),
            dma((10, 3)), dma((10, 3)), dma((10,)), dma((10,)), dma((10, 3)), dma((10, 3)),
            dma((8,)), dma((8,)), dma((16,)), dma((16,)),
        ],
        compiler_params=pltpu.CompilerParams(
            collective_id=0, has_side_effects=True, vmem_limit_bytes=62 * 2**20
        ),
        name="step",
    )(wave_coef, jnp.transpose(projector, (1, 0, 2)), occupation.reshape(1, bands), species,
      jnp.transpose(layer_in, (2, 0, 1)), bias_in.reshape(-1, 1, HID), layer_out.reshape(-1, 1, HID))
    step = 512
    return pl.pallas_call(
        correct_kernel,
        grid=(gs // step,),
        out_shape=jax.ShapeDtypeStruct((bands, gs), BF16),
        in_specs=[pl.BlockSpec((bands, 16 * SLOT), lambda t: (0, 0)), pl.BlockSpec((16 * SLOT, step), lambda t: (0, t))],
        out_specs=pl.BlockSpec((bands, step), lambda t: (0, t)),
        compiler_params=pltpu.CompilerParams(vmem_limit_bytes=40 * 2**20),
        name="correct",
    )(applied, table)


def solution(mesh):
    in_specs = (P("band", "ga"), P("band", None, "ga"), P("band"), P(), P(), P(), P())
    out_specs = P("band", "ga")
    return jax.shard_map(body, mesh=mesh, in_specs=in_specs, out_specs=out_specs, check_vma=False)
```

time: 142 us -> 117 us (0.82)
  Pallas kernels: 133 us -> 115 us
  local copies, waits for them, and re-layouts: 9.27 us -> 1.49 us
    pallas_call x1 -> x2, Pallas kernels: 133 us -> 115 us  [the longest x1 102 us: body(): pl.pallas_call(functools.partial(body_kernel, bands_all), out_shape=[jax....]
    unnamed x5 -> x2, local copies, waits for them, and re-layouts: 8.05 us -> 1.49 us
where the time goes in v2:
time: 117 us; the launch traced here: 116 us
  Pallas kernels  115 us (98%)
  local copies, waits for them, and re-layouts  1.49 us (1%)
    pallas_call x1, Pallas kernels, body(): pl.pallas_call(functools.partial(body_kernel, bands_all), out_shape=[jax....  102 us
    pallas_call x1, Pallas kernels, body(): pl.pallas_call(correct_kernel, grid=(gs // step,), out_shape=jax.ShapeDty...  13.3 us

profile of v2, /device:TPU:1, one launch (start us, length us, event | category | flops | bytes accessed | tf_op | source)
XLA Modules:
  0.0 116.4 jit_solution(11732708107501676417)
XLA Ops:
  0.0 101.6 %step.1 = (bf16[512,1792]{1,0:T(8,128)(2,1)}, bf16[1792,4096]{1,0:T(8,128)(2,1)}) custom-call(bf16[512,4096]{1,0:T(8,128)(2,1)} %w_hbm.1, bf16[27,4,4096]{2,1,0:T(4,128)(2,1)} %bitcast.6, f32[1,512]{1,0:T(1,128)} %bitcast.7, s32[64]{0:T(128)} %species_ref.1, f32[100,4,729]{2,1,0:T(4,128)} %bitcast.5, f32[4,1,100]{2,1,0:T(1,128)} %bitcast.8, f32[4,1,100]{2,1,0:T(1,128)} %bitcast.9), custom_call_target="tpu_custom_call" | custom-call | tf_op jit(solution)/shard_map/step/pallas_call | solution.py:418
  101.6 0.0 copy-start
  101.6 1.5 %copy-done = bf16[512,1792]{1,0:T(8,128)(2,1)S(1)} copy-done((bf16[512,1792]{1,0:T(8,128)(2,1)S(1)}, bf16[512,1792]{1,0:T(8,128)(2,1)}, u32[]{:S(2)}) %copy-start) | copy-done | bytes 1835032
  103.1 13.3 %correct.1 = bf16[512,4096]{1,0:T(8,128)(2,1)} custom-call(bf16[512,1792]{1,0:T(8,128)(2,1)S(1)} %copy-done, bf16[1792,4096]{1,0:T(8,128)(2,1)} %get-tuple-element.8.tab_ref), custom_call_target="tpu_custom_call" | custom-call | tf_op jit(solution)/shard_map/correct/pallas_call | solution.py:455
Async XLA Ops:
  101.6 1.5 %copy-start = (bf16[512,1792]{1,0:T(8,128)(2,1)S(1)}, bf16[512,1792]{1,0:T(8,128)(2,1)}, u32[]{:S(2)}) copy-start(bf16[512,1792]{1,0:T(8,128)(2,1)} %get-tuple-element.7.app_ref) | copy-start | bytes 5505028

commit v3 on v2

--- a/solution.py
+++ b/solution.py
@@ -21,13 +21,24 @@
 
 ORDER = ((0, 0), (0, 3), (0, 1), (1, 0), (1, 3), (1, 1), (0, 2), (1, 2))
 
-PIECES = tuple((i, 0, PAIR) for i in range(7)) + ((7, 0, 80), (7, 144, 80), (7, 80, 64))
+SPLIT = (1, 2, 4, 5, 7)
+PIECES = []
+EARLY, LATE = {}, {}
+for _i in range(8):
+    if _i in SPLIT:
+        EARLY[_i] = (len(PIECES), len(PIECES) + 1)
+        LATE[_i] = (len(PIECES) + 2,)
+        PIECES += [(_i, 0, 80), (_i, 144, 80), (_i, 80, 64)]
+    else:
+        EARLY[_i] = (len(PIECES),)
+        PIECES += [(_i, 0, PAIR)]
+NP = len(PIECES)
 
 TREE = (
     ("z10", 32, 80), ("x10", 0, 32),
-    ("z03", 32, 80), ("x03", 0, 32), ("z01", 32, 80), ("x01", 0, 32),
+    ("z03a", 32, 48), ("z03b", 80, 32), ("x03", 0, 32), ("z01a", 32, 48), ("z01b", 80, 32), ("x01", 0, 32),
     ("x02a", 0, 16), ("x02b", 16, 16), ("z02a", 32, 48), ("z02b", 80, 32),
-    ("z13", 32, 80), ("z11", 32, 80), ("x13", 0, 32), ("x11", 0, 32),
+    ("z13a", 32, 48), ("z13b", 80, 32), ("z11a", 32, 48), ("z11b", 80, 32), ("x13", 0, 32), ("x11", 0, 32),
     ("x12a", 0, 16), ("x12b", 16, 16), ("z12a", 64, 16), ("z12b", 32, 32),
     ("z12c", 80, 16), ("z12d", 96, 16),
 )
@@ -119,12 +130,18 @@
         _, first, count = TREE[i]
         arrived(rows(tab, slot_row(dz, dx, 0) + row_in_slot(first, count), count), tss.at[i], tsr.at[i])
 
-    def across(i, dz, dx, first=0, count=SLOT):
+    def crossing(i, part):
+        first, count = ((0, SLOT), (0, 80), (80, 32))[part]
+        return ORDER[i], first, count, i + 8 * (part == 2)
+
+    def across(i, part=0):
+        (dz, dx), first, count, sem = crossing(i, part)
         ref = rows(tab, slot_row(dz, dx, 0) + row_in_slot(first, count), count)
-        remote(ref, ref, d2s.at[i], d2r.at[i], at(dc=1))
-
-    def across_wait(i, dz, dx, first=0, count=SLOT):
-        arrived(rows(tab, slot_row(dz, dx, 1) + row_in_slot(first, count, 1), count), d2s.at[i], d2r.at[i])
+        remote(ref, ref, d2s.at[sem], d2r.at[sem], at(dc=1))
+
+    def across_wait(i, part=0):
+        (dz, dx), first, count, sem = crossing(i, part)
+        arrived(rows(tab, slot_row(dz, dx, 1) + row_in_slot(first, count, 1), count), d2s.at[sem], d2r.at[sem])
 
     flushes = []
 
@@ -136,7 +153,7 @@
 
     right, left, over = at(dx=1), at(dx=3), at(dz=1)
 
-    def project(*pieces):
+    def project(pieces):
         i = PIECES[pieces[0]][0]
         base = pair_row(*ORDER[i])
 
@@ -178,124 +195,207 @@
         i, first, count = PIECES[s]
         return pl.ds(pl.multiple_of(pair_row(*ORDER[i]) + first, 16), count)
 
+    def direct(s):
+        return PIECES[s][0] == 7
+
+    def block(s, dy):
+        lanes = pl.ds(pl.multiple_of(((y + dy) % 4) * 128, 128), 128)
+        return cfull.at[in_full(s), lanes]
+
     def reduce_z(s):
         i, first, count = PIECES[s]
         here = pl.ds(first, count)
         arrived(zr.at[i, here], zss.at[s], zsr.at[s])
         cfull[in_full(s), mine] = (part[i, here, mine] + zr[i, here].astype(F32)).astype(BF16)
-        for dy in (2, 1, 3):
-            ref = cfull.at[in_full(s), mine]
-            remote(ref, ref, ags.at[s, 3 - dy], agr.at[s, 3 - dy], at(dy=dy))
+        for dy in (2, 1, 3) if direct(s) else (1, 3):
+            remote(block(s, 0), block(s, 0), ags.at[s, 3 - dy], agr.at[s, 3 - dy], at(dy=dy))
+
+    def relay(s):
+        for dy in (1, 3):
+            arrived(block(s, dy), ags.at[s, dy - 1], agr.at[s, dy - 1])
+        dy = 1 + 2 * (s % 2)
+        remote(block(s, dy), block(s, dy), ags.at[s, 1], agr.at[s, 1], at(dy=4 - dy))
 
     def gathered(s):
-        for dy in range(1, 4):
-            lanes = pl.ds(pl.multiple_of(((y + dy) % 4) * 128, 128), 128)
-            arrived(cfull.at[in_full(s), lanes], ags.at[s, dy - 1], agr.at[s, dy - 1])
+        for dy in (1, 2, 3) if direct(s) else (2,):
+            arrived(block(s, dy), ags.at[s, dy - 1], agr.at[s, dy - 1])
 
     tree_send("z10", 0, 0, over)
     tree_send("x03", 0, 0, right)
     tree_send("x01", 0, 0, left)
-    across(0, 0, 0)
-    tree_send("z03", 0, 0, right)
-    tree_send("z01", 0, 0, left)
-    tree_send("x10", 0, 0, over)
-
+    across(0)
+    tree_send("z03a", 0, 0, right)
+    tree_send("z01a", 0, 0, left)
+    tree_send("z03b", 0, 0, right)
+    tree_send("z01b", 0, 0, left)
     wcopy.wait()
-    across_wait(0, 0, 0)
-    project(0)
+    across_wait(0)
+    project(EARLY[0])
     flush(0)
     tree_wait("x03", 0, 3)
     tree_send("x02a", 0, 3, right)
-    tree_send("x13", 0, 3, over)
     tree_wait("x01", 0, 1)
     tree_send("x02b", 0, 1, left)
+    for s in EARLY[0]:
+        reduce_y(s)
+    tree_send("x10", 0, 0, over)
+    tree_send("x13", 0, 3, over)
     tree_send("x11", 0, 1, over)
-    reduce_y(0)
-
     lcopy.wait()
     for kind in range(SPECIES):
         lin[kind] = lraw[:, kind, :].T
-
+    tree_wait("z03a", 0, 3)
+    across(1, 1)
+    tree_wait("z01a", 0, 1)
+    across(2, 1)
     tree_wait("z10", 1, 0)
-    tree_send("z13", 1, 0, right)
-    tree_send("z11", 1, 0, left)
-    tree_wait("z03", 0, 3)
+    tree_send("z13a", 1, 0, right)
+    tree_send("z11a", 1, 0, left)
+    tree_send("z13b", 1, 0, right)
+    tree_send("z11b", 1, 0, left)
     tree_send("z02a", 0, 3, right)
-    across(1, 0, 3)
-    tree_wait("z01", 0, 1)
+    for s in EARLY[0]:
+        reduce_z(s)
+    across_wait(1, 1)
+    project(EARLY[1])
+    across_wait(2, 1)
+    project(EARLY[2])
+    tree_wait("z03b", 0, 3)
+    across(1, 2)
+    tree_wait("z01b", 0, 1)
     tree_send("z02b", 0, 1, left)
-    across(2, 0, 1)
+    across(2, 2)
     tree_wait("x10", 1, 0)
-    across(3, 1, 0)
+    across(3)
+    across_wait(1, 2)
+    project(LATE[1])
+    for s in EARLY[0]:
+        relay(s)
+    for s in EARLY[1]:
+        reduce_y(s)
+    across_wait(2, 2)
+    project(LATE[2])
+    for s in EARLY[2]:
+        reduce_y(s)
+    across_wait(3)
+    project(EARLY[3])
+    flush(1)
+    flush(2)
+    flush(3)
+    for s in LATE[1]:
+        reduce_y(s)
+    for s in LATE[2]:
+        reduce_y(s)
     tree_wait("x02a", 0, 2)
+    tree_wait("x02b", 0, 2)
     tree_send("x12a", 0, 2, over)
-    tree_wait("x02b", 0, 2)
     tree_send("x12b", 0, 2, over)
-    across_wait(1, 0, 3)
-    project(1)
-    across_wait(2, 0, 1)
-    project(2)
-    across_wait(3, 1, 0)
-    project(3)
-    for i in (1, 2, 3):
-        flush(i)
-    reduce_z(0)
-    reduce_y(1)
-    reduce_y(2)
-    reduce_y(3)
-
-    tree_wait("z13", 1, 3)
+    tree_wait("z13a", 1, 3)
     tree_send("z12a", 1, 3, right)
+    tree_wait("z11a", 1, 1)
+    tree_send("z12b", 1, 1, left)
+    tree_wait("x13", 1, 3)
+    across(4, 1)
+    tree_wait("x11", 1, 1)
+    across(5, 1)
+    for s in EARLY[3]:
+        reduce_y(s)
+    across_wait(4, 1)
+    project(EARLY[4])
+    across_wait(5, 1)
+    project(EARLY[5])
+    for s in EARLY[1]:
+        reduce_z(s)
+    for s in EARLY[2]:
+        reduce_z(s)
+    tree_wait("z13b", 1, 3)
     tree_send("z12c", 1, 3, right)
-    tree_wait("z11", 1, 1)
-    tree_send("z12b", 1, 1, left)
+    across(4, 2)
+    tree_wait("z11b", 1, 1)
     tree_send("z12d", 1, 1, left)
-    tree_wait("x13", 1, 3)
-    across(4, 1, 3)
-    tree_wait("x11", 1, 1)
-    across(5, 1, 1)
-    reduce_z(1)
-    across_wait(4, 1, 3)
-    project(4)
-    across_wait(5, 1, 1)
-    project(5)
+    across(5, 2)
+    for s in LATE[1]:
+        reduce_z(s)
+    for s in LATE[2]:
+        reduce_z(s)
+    across_wait(4, 2)
+    project(LATE[4])
+    for s in EARLY[4]:
+        reduce_y(s)
+    across_wait(5, 2)
+    project(LATE[5])
+    for s in EARLY[5]:
+        reduce_y(s)
+    for s in EARLY[3]:
+        reduce_z(s)
+    for s in EARLY[1]:
+        relay(s)
+    for s in EARLY[2]:
+        relay(s)
     flush(4)
     flush(5)
-    reduce_z(2)
-    reduce_z(3)
-    reduce_y(4)
-
     tree_wait("z02a", 0, 2)
+    across(6, 1)
     tree_wait("z02b", 0, 2)
-    across(6, 0, 2)
-    reduce_y(5)
-    across_wait(6, 0, 2)
-    project(6)
+    across(6, 2)
+    for s in LATE[4]:
+        reduce_y(s)
+    for s in LATE[5]:
+        reduce_y(s)
+    for s in LATE[1]:
+        relay(s)
+    for s in LATE[2]:
+        relay(s)
+    for s in EARLY[4]:
+        reduce_z(s)
+    across_wait(6, 1)
+    across_wait(6, 2)
+    project(EARLY[6])
     flush(6)
-    reduce_z(4)
-    reduce_z(5)
+    for s in EARLY[5]:
+        reduce_z(s)
+    for s in EARLY[3]:
+        relay(s)
     tree_wait("x12a", 1, 2)
     tree_wait("x12b", 1, 2)
     tree_wait("z12a", 1, 2)
     tree_wait("z12b", 1, 2)
-    across(7, 1, 2, 0, 80)
-    across_wait(7, 1, 2, 0, 80)
-    project(7, 8)
+    across(7, 1)
+    for s in LATE[4]:
+        reduce_z(s)
+    for s in LATE[5]:
+        reduce_z(s)
+    across_wait(7, 1)
+    project(EARLY[7])
     tree_wait("z12c", 1, 2)
     tree_wait("z12d", 1, 2)
-    across(8, 1, 2, 80, 32)
-    across_wait(8, 1, 2, 80, 32)
-    project(9)
+    across(7, 2)
+    for s in EARLY[6]:
+        reduce_y(s)
+    for s in EARLY[4]:
+        relay(s)
+    for s in EARLY[5]:
+        relay(s)
+    across_wait(7, 2)
+    project(LATE[7])
     flush(7)
-    reduce_y(6)
-    reduce_y(7)
-    reduce_y(8)
-    reduce_y(9)
-    reduce_z(6)
-    reduce_z(7)
-    reduce_z(8)
-    reduce_z(9)
-    for s in range(10):
+    for s in EARLY[7]:
+        reduce_y(s)
+    for s in LATE[4]:
+        relay(s)
+    for s in LATE[5]:
+        relay(s)
+    for s in LATE[7]:
+        reduce_y(s)
+    for s in EARLY[6]:
+        reduce_z(s)
+    for s in EARLY[7]:
+        reduce_z(s)
+    for s in LATE[7]:
+        reduce_z(s)
+    for s in EARLY[6]:
+        relay(s)
+    for s in range(NP):
         gathered(s)
 
     lane_atom = lax.broadcasted_iota(jnp.int32, (KP, SLOT), 1) % 4
@@ -390,20 +490,17 @@
     def turn(j, carry):
         block = pl.ds(pl.multiple_of(j * 256, 256), 256)
         app[:, block] = appt[block, :].T
+        pltpu.make_async_copy(app.at[:, block], app_out.at[:, block], apps.at[j]).start()
         return carry
 
     lax.fori_loop(0, 7, turn, 0)
-    last = pltpu.make_async_copy(app, app_out, apps)
-    last.start()
-    last.wait()
+    for j in range(7):
+        block = pl.ds(j * 256, 256)
+        pltpu.make_async_copy(app.at[:, block], app_out.at[:, block], apps.at[j]).wait()
     for copy in flushes:
         copy.wait()
     for copy in sends:
         copy.wait_send()
-
-
-def correct_kernel(app_ref, tab_ref, out_ref):
-    out_ref[...] = jnp.dot(app_ref[...], tab_ref[...], preferred_element_type=F32).astype(BF16)
 
 
 def body(wave_coef, projector, occupation, species, layer_in, bias_in, layer_out):
@@ -441,8 +538,8 @@
             pltpu.VMEM((bands, 16 * SLOT), BF16),
             pltpu.VMEM((SLOT, 128), F32),
             pltpu.VMEM((16, SLOT, 128), F32),
-            dma((3,)), dma((8,)), dma, dma((NT,)), dma((NT,)), dma((9,)), dma((9,)),
-            dma((10, 3)), dma((10, 3)), dma((10,)), dma((10,)), dma((10, 3)), dma((10, 3)),
+            dma((3,)), dma((8,)), dma((7,)), dma((NT,)), dma((NT,)), dma((16,)), dma((16,)),
+            dma((NP, 3)), dma((NP, 3)), dma((NP,)), dma((NP,)), dma((NP, 3)), dma((NP, 3)),
             dma((8,)), dma((8,)), dma((16,)), dma((16,)),
         ],
         compiler_params=pltpu.CompilerParams(
@@ -451,16 +548,7 @@
         name="step",
     )(wave_coef, jnp.transpose(projector, (1, 0, 2)), occupation.reshape(1, bands), species,
       jnp.transpose(layer_in, (2, 0, 1)), bias_in.reshape(-1, 1, HID), layer_out.reshape(-1, 1, HID))
-    step = 512
-    return pl.pallas_call(
-        correct_kernel,
-        grid=(gs // step,),
-        out_shape=jax.ShapeDtypeStruct((bands, gs), BF16),
-        in_specs=[pl.BlockSpec((bands, 16 * SLOT), lambda t: (0, 0)), pl.BlockSpec((16 * SLOT, step), lambda t: (0, t))],
-        out_specs=pl.BlockSpec((bands, step), lambda t: (0, t)),
-        compiler_params=pltpu.CompilerParams(vmem_limit_bytes=40 * 2**20),
-        name="correct",
-    )(applied, table)
+    return jnp.dot(applied, table, preferred_element_type=F32).astype(BF16)
 
 
 def solution(mesh):

time: 117 us -> 112 us (0.957)
  Pallas kernels: 115 us -> 98.5 us
  matrix products: 0 us -> 13 us
  local copies, waits for them, and re-layouts: 1.49 us -> 0 us
    pallas_call x1 -> x0, Pallas kernels: 13.3 us -> none  [body(): pl.pallas_call(correct_kernel, grid=(gs // step,), out_shape=jax.ShapeDty...]
    dot_general x0 -> x1, matrix products: none -> 13 us  [body(): return jnp.dot(applied, table, preferred_element_type=F32).astype(BF16)]
    pallas_call x1, Pallas kernels: 102 us -> 98.5 us  [body(): pl.pallas_call(functools.partial(body_kernel, bands_all), out_shape=[jax....]
    unnamed x2 -> x0, local copies, waits for them, and re-layouts: 1.49 us -> none
where the time goes in v3:
time: 112 us
  Pallas kernels  98.5 us (88%)
  matrix products  13 us (12%)
    pallas_call x1, Pallas kernels, body(): pl.pallas_call(functools.partial(body_kernel, bands_all), out_shape=[jax....  98.5 us
    dot_general x1, matrix products, body(): return jnp.dot(applied, table, preferred_element_type=F32).astype(BF16)  13 us

profile of v3, /device:TPU:1, one launch (start us, length us, event | category | flops | bytes accessed | tf_op | source)
XLA Modules:
  0.0 111.5 jit_solution(11467299125354836907)
XLA Ops:
  0.0 98.5 %step.1 = (bf16[512,1792]{1,0:T(8,128)(2,1)}, bf16[1792,4096]{1,0:T(8,128)(2,1)}) custom-call(bf16[512,4096]{1,0:T(8,128)(2,1)} %w_hbm.1, bf16[27,4,4096]{2,1,0:T(4,128)(2,1)} %bitcast.8, f32[1,512]{1,0:T(1,128)} %bitcast.9, s32[64]{0:T(128)} %species_ref.1, f32[100,4,729]{2,1,0:T(4,128)} %bitcast.7, f32[4,1,100]{2,1,0:T(1,128)} %bitcast.10, ...), custom_call_target="tpu_custom_call" | custom-call | tf_op jit(solution)/shard_map/step/pallas_call | solution.py:515
  98.5 13.0 %convolution_convert_fusion = bf16[512,4096]{1,0:T(8,128)(2,1)} fusion(bf16[512,1792]{1,0:T(8,128)(2,1)} %get-tuple-element.7, bf16[1792,4096]{1,0:T(8,128)(2,1)} %get-tuple-element.8), kind=kOutput, calls=%fused_computation | convolution fusion | flops 7518289920 | bytes 20709376 | tf_op jit(solution)/shard_map/dot_general | solution.py:551

commit v4 on v3

--- a/solution.py
+++ b/solution.py
@@ -46,9 +46,9 @@
 NT = len(TREE)
 
 
-def body_kernel(bands_all, w_hbm, p_hbm, occ_ref, species_ref, lin_hbm, bias_ref, lout_ref, app_out,
-                tab_out, w, tab, pin, lraw, part, part16, ry, zs, zr, cfull, lin, dsend, dpart, drecv, xs, xall, appt, app, bd, bds,
-                lsem, tabs, apps, tss, tsr, d2s, d2r, rys, ryr, zss, zsr, ags, agr, dens_s, dens_r, xss, xsr):
+def body_kernel(bands_all, w_hbm, p_hbm, occ_ref, species_ref, lin_hbm, bias_ref, lout_ref, out_ref,
+                w, tab, pin, lraw, part, part16, ry, zs, zr, cfull, lin, dsend, dpart, drecv, xs, xall, appt, app, bd, bds,
+                lsem, tss, tsr, d2s, d2r, rys, ryr, zss, zsr, ags, agr, dens_s, dens_r, xss, xsr):
     band = lax.axis_index("band")
     ga = lax.axis_index("ga")
     zh, x, c = band // 8, (band // 2) % 4, band % 2
@@ -143,14 +143,6 @@
         (dz, dx), first, count, sem = crossing(i, part)
         arrived(rows(tab, slot_row(dz, dx, 1) + row_in_slot(first, count, 1), count), d2s.at[sem], d2r.at[sem])
 
-    flushes = []
-
-    def flush(i):
-        ref = rows(tab, pair_row(*ORDER[i]), PAIR)
-        copy = pltpu.make_async_copy(ref, rows(tab_out, pair_row(*ORDER[i]), PAIR), tabs.at[i])
-        copy.start()
-        flushes.append(copy)
-
     right, left, over = at(dx=1), at(dx=3), at(dz=1)
 
     def project(pieces):
@@ -231,7 +223,6 @@
     wcopy.wait()
     across_wait(0)
     project(EARLY[0])
-    flush(0)
     tree_wait("x03", 0, 3)
     tree_send("x02a", 0, 3, right)
     tree_wait("x01", 0, 1)
@@ -279,9 +270,6 @@
         reduce_y(s)
     across_wait(3)
     project(EARLY[3])
-    flush(1)
-    flush(2)
-    flush(3)
     for s in LATE[1]:
         reduce_y(s)
     for s in LATE[2]:
@@ -332,8 +320,6 @@
         relay(s)
     for s in EARLY[2]:
         relay(s)
-    flush(4)
-    flush(5)
     tree_wait("z02a", 0, 2)
     across(6, 1)
     tree_wait("z02b", 0, 2)
@@ -351,7 +337,6 @@
     across_wait(6, 1)
     across_wait(6, 2)
     project(EARLY[6])
-    flush(6)
     for s in EARLY[5]:
         reduce_z(s)
     for s in EARLY[3]:
@@ -378,7 +363,6 @@
         relay(s)
     across_wait(7, 2)
     project(LATE[7])
-    flush(7)
     for s in EARLY[7]:
         reduce_y(s)
     for s in LATE[4]:
@@ -490,15 +474,16 @@
     def turn(j, carry):
         block = pl.ds(pl.multiple_of(j * 256, 256), 256)
         app[:, block] = appt[block, :].T
-        pltpu.make_async_copy(app.at[:, block], app_out.at[:, block], apps.at[j]).start()
         return carry
 
     lax.fori_loop(0, 7, turn, 0)
-    for j in range(7):
-        block = pl.ds(j * 256, 256)
-        pltpu.make_async_copy(app.at[:, block], app_out.at[:, block], apps.at[j]).wait()
-    for copy in flushes:
-        copy.wait()
+
+    def correct(t, carry):
+        cols = pl.ds(pl.multiple_of(t * 512, 512), 512)
+        out_ref[:, cols] = jnp.dot(app[...], tab[:, cols], preferred_element_type=F32).astype(BF16)
+        return carry
+
+    lax.fori_loop(0, 8, correct, 0)
     for copy in sends:
         copy.wait_send()
 
@@ -508,15 +493,15 @@
     bands = wave_coef.shape[0]
     bands_all = bands * lax.axis_size("band")
     assert atoms_here == 4 and orbitals == K and bands == 512
-    any_space = pl.BlockSpec(memory_space=pl.ANY)
+    hbm = pl.BlockSpec(memory_space=pltpu.HBM)
     vmem = pl.BlockSpec(memory_space=pltpu.VMEM)
     smem = pl.BlockSpec(memory_space=pltpu.SMEM)
     dma = pltpu.SemaphoreType.DMA
-    applied, table = pl.pallas_call(
+    return pl.pallas_call(
         functools.partial(body_kernel, bands_all),
-        out_shape=[jax.ShapeDtypeStruct((bands, 16 * SLOT), BF16), jax.ShapeDtypeStruct((16 * SLOT, gs), BF16)],
-        in_specs=[any_space, any_space, vmem, smem, any_space, vmem, vmem],
-        out_specs=[any_space, any_space],
+        out_shape=pltpu.VMEM((bands, gs), BF16),
+        in_specs=[hbm, hbm, vmem, smem, hbm, vmem, vmem],
+        out_specs=vmem,
         scratch_shapes=[
             pltpu.VMEM((bands, gs), BF16),
             pltpu.VMEM((16 * SLOT, gs), BF16),
@@ -538,17 +523,16 @@
             pltpu.VMEM((bands, 16 * SLOT), BF16),
             pltpu.VMEM((SLOT, 128), F32),
             pltpu.VMEM((16, SLOT, 128), F32),
-            dma((3,)), dma((8,)), dma((7,)), dma((NT,)), dma((NT,)), dma((16,)), dma((16,)),
+            dma((3,)), dma((NT,)), dma((NT,)), dma((16,)), dma((16,)),
             dma((NP, 3)), dma((NP, 3)), dma((NP,)), dma((NP,)), dma((NP, 3)), dma((NP, 3)),
             dma((8,)), dma((8,)), dma((16,)), dma((16,)),
         ],
         compiler_params=pltpu.CompilerParams(
-            collective_id=0, has_side_effects=True, vmem_limit_bytes=62 * 2**20
+            collective_id=0, has_side_effects=True, vmem_limit_bytes=57 * 2**20
         ),
         name="step",
     )(wave_coef, jnp.transpose(projector, (1, 0, 2)), occupation.reshape(1, bands), species,
       jnp.transpose(layer_in, (2, 0, 1)), bias_in.reshape(-1, 1, HID), layer_out.reshape(-1, 1, HID))
-    return jnp.dot(applied, table, preferred_element_type=F32).astype(BF16)
 
 
 def solution(mesh):

time: 112 us -> 109 us (0.973)
  matrix products: 13 us -> 0 us
  Pallas kernels: 98.5 us -> 107 us
  local copies, waits for them, and re-layouts: 0 us -> 2.02 us
    dot_general x1 -> x0, matrix products: 13 us -> none  [body(): return jnp.dot(applied, table, preferred_element_type=F32).astype(BF16)]
    pallas_call x1, Pallas kernels: 98.5 us -> 107 us  [body(): pl.pallas_call(functools.partial(body_kernel, bands_all), out_shape=pltpu...]
    unnamed x0 -> x1, local copies, waits for them, and re-layouts: none -> 2.02 us
where the time goes in v4:
time: 109 us
  Pallas kernels  107 us (98%)
  local copies, waits for them, and re-layouts  2.02 us (2%)
    pallas_call x1, Pallas kernels, body(): pl.pallas_call(functools.partial(body_kernel, bands_all), out_shape=pltpu...  107 us

profile of v4, /device:TPU:1, one launch (start us, length us, event | category | flops | bytes accessed | tf_op | source)
XLA Modules:
  0.0 108.6 jit_solution(2746820158941910307)
XLA Ops:
  0.0 106.6 %step.1 = bf16[512,4096]{1,0:T(8,128)(2,1)S(1)} custom-call(bf16[512,4096]{1,0:T(8,128)(2,1)} %w_hbm.1, bf16[27,4,4096]{2,1,0:T(4,128)(2,1)} %bitcast.6, f32[1,512]{1,0:T(1,128)} %bitcast.7, s32[64]{0:T(128)} %species_ref.1, f32[100,4,729]{2,1,0:T(4,128)} %bitcast.5, f32[4,1,100]{2,1,0:T(1,128)} %bitcast.8, f32[4,1,100]{2,1,0:T(1,128)} %bitcast.9), custom_call_target="tpu_custom_call" | custom-call | tf_op jit(solution)/shard_map/step/pallas_call | solution.py:500
  106.6 2.0 %copy.9 = bf16[512,4096]{1,0:T(8,128)(2,1)} copy(bf16[512,4096]{1,0:T(8,128)(2,1)S(1)} %step.1) | data formatting | bytes 8388608

commit v5 on v4

v5 whole, which is shorter than its diff:
```python
import functools
import math

import jax
import jax.numpy as jnp
from jax import lax
from jax.experimental import pallas as pl
from jax.experimental.pallas import tpu as pltpu
from jax.sharding import PartitionSpec as P

MESH = pl.DeviceIdType.MESH
F32 = jnp.float32
BF16 = jnp.bfloat16

K = 27
KP = 28
SLOT = 4 * KP
PAIR = 2 * SLOT
HID = 100
SPECIES = 4

ORDER = ((0, 0), (0, 3), (0, 1), (1, 0), (1, 3), (1, 1), (0, 2), (1, 2))

SPLIT = (1, 2, 4, 5, 7)
TABLE_ROWS = ((0, 80), (144, 80), (80, 64))
PIECES = []
EARLY, LATE = {}, {}
for _i in range(8):
    EARLY[_i] = len(PIECES)
    if _i in SPLIT:
        LATE[_i] = EARLY[_i] + 1
        PIECES += [(_i, 0, 160), (_i, 160, 64)]
    else:
        PIECES += [(_i, 0, PAIR)]
NP = len(PIECES)
POOL = 64

TREE = (
    ("z10", 32, 80), ("x10", 0, 32),
    ("z03a", 32, 48), ("z03b", 80, 32), ("x03", 0, 32), ("z01a", 32, 48), ("z01b", 80, 32), ("x01", 0, 32),
    ("x02a", 0, 16), ("x02b", 16, 16), ("z02a", 32, 48), ("z02b", 80, 32),
    ("z13a", 32, 48), ("z13b", 80, 32), ("z11a", 32, 48), ("z11b", 80, 32), ("x13", 0, 32), ("x11", 0, 32),
    ("x12a", 0, 16), ("x12b", 16, 16), ("z12a", 64, 16), ("z12b", 32, 32),
    ("z12c", 80, 16), ("z12d", 96, 16),
)
TREE_ID = {name: i for i, (name, _, _) in enumerate(TREE)}
NT = len(TREE)


def body_kernel(bands_all, w_hbm, p_hbm, occ_ref, species_ref, lin_hbm, bias_ref, lout_ref, app, tab,
                w, pin, lraw, part, part16, ry, zs, zr, cfull, lin, dsend, dpart, drecv, xs, xall, appt, bd, bds,
                lsem, pool, tsr, d2r, ryr, zsr, agr, dens_r, xsr):
    band = lax.axis_index("band")
    ga = lax.axis_index("ga")
    zh, x, c = band // 8, (band // 2) % 4, band % 2
    y, zl = ga // 2, ga % 2

    def at(dz=0, dx=0, dc=0, dy=0, dl=0):
        nzh, nx, nc = (zh + dz) % 2, (x + dx) % 4, (c + dc) % 2
        ny, nzl = (y + dy) % 4, (zl + dl) % 2
        return (nzh * 8 + nx * 2 + nc, ny * 2 + nzl)

    def slot_row(dz, dx, dc):
        nzh, nx, nc = (zh + dz) % 2, (x + dx) % 4, (c + dc) % 2
        return (nzh * 8 + nx * 2 + nc) * SLOT

    def pair_row(dz, dx):
        return (((zh + dz) % 2) * 4 + (x + dx) % 4) * PAIR

    def row_in_slot(first, count, dc=0):
        return jnp.where((c + dc) % 2 == 0, first, SLOT - first - count)

    def rows(ref, start, count):
        return ref.at[pl.ds(pl.multiple_of(start, 16), count)]

    wcopy = pltpu.make_async_copy(w_hbm, w, lsem.at[0])
    own_row = slot_row(0, 0, 0)
    pcopy = pltpu.make_async_copy(p_hbm, pin, lsem.at[1])
    lcopy = pltpu.make_async_copy(lin_hbm, lraw, lsem.at[2])
    pcopy.start()
    wcopy.start()
    lcopy.start()

    barrier = pltpu.get_barrier_semaphore()
    partners = [at(dc=1)]
    for dz in range(2):
        for dx in range(4):
            if dz or dx:
                partners.append(at(dz=dz, dx=dx))
    for dy in range(4):
        for dl in range(2):
            if dy or dl:
                partners.append(at(dy=dy, dl=dl))
                partners.append(at(dy=dy, dl=dl, dc=1))
    for partner in partners:
        pl.semaphore_signal(barrier, inc=1, device_id=partner, device_id_type=MESH)
    pcopy.wait()

    def pack(t, carry):
        cols = pl.ds(pl.multiple_of(t * 512, 512), 512)
        flat = pin[:, :, cols].astype(F32).reshape(4 * K, 512)
        full = jnp.concatenate([flat, jnp.zeros((SLOT - 4 * K, 512), F32)], axis=0)
        tab[pl.ds(pl.multiple_of(own_row, 16), SLOT), cols] = full.astype(BF16)
        return carry

    lax.fori_loop(0, 8, pack, 0)
    pl.semaphore_wait(barrier, len(partners))

    sends = []

    def remote(src, dst, rs, device):
        n = len(sends)
        if n >= POOL:
            sends[n - POOL].wait_send()
        copy = pltpu.make_async_remote_copy(
            src_ref=src, dst_ref=dst, send_sem=pool.at[n % POOL], recv_sem=rs, device_id=device, device_id_type=MESH
        )
        copy.start()
        sends.append(copy)

    def arrived(dst, rs):
        pltpu.make_async_remote_copy(
            src_ref=dst, dst_ref=dst, send_sem=pool.at[0], recv_sem=rs, device_id=at(dc=1), device_id_type=MESH
        ).wait_recv()

    def tree_send(name, dz, dx, device):
        i = TREE_ID[name]
        _, first, count = TREE[i]
        ref = rows(tab, slot_row(dz, dx, 0) + row_in_slot(first, count), count)
        remote(ref, ref, tsr.at[i], device)

    def tree_wait(name, dz, dx):
        i = TREE_ID[name]
        _, first, count = TREE[i]
        arrived(rows(tab, slot_row(dz, dx, 0) + row_in_slot(first, count), count), tsr.at[i])

    def crossing(i, part):
        first, count = ((0, SLOT), (0, 80), (80, 32))[part]
        return ORDER[i], first, count, i + 8 * (part == 2)

    def across(i, part=0):
        (dz, dx), first, count, sem = crossing(i, part)
        ref = rows(tab, slot_row(dz, dx, 0) + row_in_slot(first, count), count)
        remote(ref, ref, d2r.at[sem], at(dc=1))

    def across_wait(i, part=0):
        (dz, dx), first, count, sem = crossing(i, part)
        arrived(rows(tab, slot_row(dz, dx, 1) + row_in_slot(first, count, 1), count), d2r.at[sem])

    right, left, over = at(dx=1), at(dx=3), at(dz=1)

    def project(s):
        i, first, count = PIECES[s]
        base = pair_row(*ORDER[i])

        def read(start, size):
            return tab[pl.ds(pl.multiple_of(base + start, 16), size), :]

        def half(t, carry):
            cols = pl.ds(pl.multiple_of(t * 256, 256), 256)

            def times(table):
                return lax.dot_general(table, w[cols, :], (((1,), (1,)), ((), ())), preferred_element_type=F32)

            def keep(to, got):
                part[i, to:to + got.shape[0], cols] = got
                part16[i, to:to + got.shape[0], cols] = got.astype(BF16)

            if count == PAIR:
                got = times(read(0, PAIR))
                to = 0
                for start, size in TABLE_ROWS:
                    keep(to, got[start:start + size])
                    to += size
            elif first == 0:
                keep(0, times(jnp.concatenate([read(*span) for span in TABLE_ROWS[:2]], axis=0)))
            else:
                keep(first, times(read(*TABLE_ROWS[2])))
            return carry

        lax.fori_loop(0, 2, half, 0)
        here = pl.ds(first, count)
        for dy in (2, 1, 3):
            lanes = pl.ds(pl.multiple_of(((y + dy) % 4) * 128, 128), 128)
            remote(part16.at[i, here, lanes], ry.at[i, 3 - dy, here], ryr.at[s], at(dy=dy))

    mine = pl.ds(pl.multiple_of(y * 128, 128), 128)

    def reduce_y(s):
        i, first, count = PIECES[s]
        here = pl.ds(first, count)
        total = part[i, here, mine]
        arrived(ry.at[i, :, here], ryr.at[s])
        for j in range(3):
            total = total + ry[i, j, here].astype(F32)
        part[i, here, mine] = total
        zs[i, here] = total.astype(BF16)
        remote(zs.at[i, here], zr.at[i, here], zsr.at[s], at(dl=1))

    def direct(s):
        return PIECES[s][0] == 7

    def block_at(s, dy):
        i, first, count = PIECES[s]
        lanes = pl.ds(pl.multiple_of(((y + dy) % 4) * 128, 128), 128)
        return pl.ds(pl.multiple_of(pair_row(*ORDER[i]) + first, 16), count), lanes

    def block(s, dy):
        return cfull.at[block_at(s, dy)]

    def reduce_z(s):
        i, first, count = PIECES[s]
        here = pl.ds(first, count)
        arrived(zr.at[i, here], zsr.at[s])
        cfull[block_at(s, 0)] = (part[i, here, mine] + zr[i, here].astype(F32)).astype(BF16)
        for dy in (2, 1, 3) if direct(s) else (1, 3):
            remote(block(s, 0), block(s, 0), agr.at[s, 3 - dy], at(dy=dy))

    def relay(s):
        for dy in (1, 3):
            arrived(block(s, dy), agr.at[s, dy - 1])
        dy = 1 + 2 * (s % 2)
        remote(block(s, dy), block(s, dy), agr.at[s, 1], at(dy=4 - dy))

    def gathered(s):
        for dy in (1, 2, 3) if direct(s) else (2,):
            arrived(block(s, dy), agr.at[s, dy - 1])

    def coef_of(pair, h):
        cuts = ((0, 80), (160, 32)) if h == 0 else ((192, 32), (80, 80))
        return jnp.concatenate([cfull[pl.ds(pl.multiple_of(pair * PAIR + a, 16), n), :] for a, n in cuts], axis=0)

    tree_send("z10", 0, 0, over)
    tree_send("x03", 0, 0, right)
    tree_send("x01", 0, 0, left)
    across(0)
    tree_send("z03a", 0, 0, right)
    tree_send("z01a", 0, 0, left)
    tree_send("z03b", 0, 0, right)
    tree_send("z01b", 0, 0, left)
    wcopy.wait()
    across_wait(0)
    project(EARLY[0])
    tree_wait("x03", 0, 3)
    tree_send("x02a", 0, 3, right)
    tree_wait("x01", 0, 1)
    tree_send("x02b", 0, 1, left)
    reduce_y(EARLY[0])
    tree_send("x10", 0, 0, over)
    tree_send("x13", 0, 3, over)
    tree_send("x11", 0, 1, over)
    lcopy.wait()
    for kind in range(SPECIES):
        lin[kind] = lraw[:, kind, :].T
    tree_wait("z03a", 0, 3)
    across(1, 1)
    tree_wait("z01a", 0, 1)
    across(2, 1)
    tree_wait("z10", 1, 0)
    tree_send("z13a", 1, 0, right)
    tree_send("z11a", 1, 0, left)
    tree_send("z13b", 1, 0, right)
    tree_send("z11b", 1, 0, left)
    tree_send("z02a", 0, 3, right)
    reduce_z(EARLY[0])
    across_wait(1, 1)
    project(EARLY[1])
    across_wait(2, 1)
    project(EARLY[2])
    tree_wait("z03b", 0, 3)
    across(1, 2)
    tree_wait("z01b", 0, 1)
    tree_send("z02b", 0, 1, left)
    across(2, 2)
    tree_wait("x10", 1, 0)
    across(3)
    across_wait(1, 2)
    project(LATE[1])
    relay(EARLY[0])
    reduce_y(EARLY[1])
    across_wait(2, 2)
    project(LATE[2])
    reduce_y(EARLY[2])
    across_wait(3)
    project(EARLY[3])
    reduce_y(LATE[1])
    reduce_y(LATE[2])
    tree_wait("x02a", 0, 2)
    tree_wait("x02b", 0, 2)
    tree_send("x12a", 0, 2, over)
    tree_send("x12b", 0, 2, over)
    tree_wait("z13a", 1, 3)
    tree_send("z12a", 1, 3, right)
    tree_wait("z11a", 1, 1)
    tree_send("z12b", 1, 1, left)
    tree_wait("x13", 1, 3)
    across(4, 1)
    tree_wait("x11", 1, 1)
    across(5, 1)
    reduce_y(EARLY[3])
    across_wait(4, 1)
    project(EARLY[4])
    across_wait(5, 1)
    project(EARLY[5])
    reduce_z(EARLY[1])
    reduce_z(EARLY[2])
    tree_wait("z13b", 1, 3)
    tree_send("z12c", 1, 3, right)
    across(4, 2)
    tree_wait("z11b", 1, 1)
    tree_send("z12d", 1, 1, left)
    across(5, 2)
    reduce_z(LATE[1])
    reduce_z(LATE[2])
    across_wait(4, 2)
    project(LATE[4])
    reduce_y(EARLY[4])
    across_wait(5, 2)
    project(LATE[5])
    reduce_y(EARLY[5])
    reduce_z(EARLY[3])
    relay(EARLY[1])
    relay(EARLY[2])
    tree_wait("z02a", 0, 2)
    across(6, 1)
    tree_wait("z02b", 0, 2)
    across(6, 2)
    reduce_y(LATE[4])
    reduce_y(LATE[5])
    relay(LATE[1])
    relay(LATE[2])
    reduce_z(EARLY[4])
    across_wait(6, 1)
    across_wait(6, 2)
    project(EARLY[6])
    reduce_z(EARLY[5])
    relay(EARLY[3])
    tree_wait("x12a", 1, 2)
    tree_wait("x12b", 1, 2)
    tree_wait("z12a", 1, 2)
    tree_wait("z12b", 1, 2)
    across(7, 1)
    reduce_z(LATE[4])
    reduce_z(LATE[5])
    across_wait(7, 1)
    project(EARLY[7])
    tree_wait("z12c", 1, 2)
    tree_wait("z12d", 1, 2)
    across(7, 2)
    across_wait(7, 2)
    project(LATE[7])
    reduce_y(EARLY[6])
    relay(EARLY[4])
    relay(EARLY[5])
    reduce_y(EARLY[7])
    reduce_y(LATE[7])
    relay(LATE[4])
    relay(LATE[5])
    reduce_z(EARLY[6])
    reduce_z(EARLY[7])
    reduce_z(LATE[7])
    relay(EARLY[6])
    for s in range(NP):
        gathered(s)

    lane_atom = lax.broadcasted_iota(jnp.int32, (KP, SLOT), 1) % 4
    occ = occ_ref[...]
    for h in range(2):
        coef = coef_of(ga, h)
        weighted = coef.astype(F32) * occ
        high = weighted.astype(BF16)
        low = (weighted - high.astype(F32)).astype(BF16)
        dims = (((1,), (1,)), ((), ()))
        gram = lax.dot_general(high, coef, dims, preferred_element_type=F32) + lax.dot_general(
            low, coef, dims, preferred_element_type=F32
        )
        bd[:, 0:SLOT] = gram
        packed = jnp.zeros((KP, SLOT), F32)
        for a in range(4):
            packed = packed + jnp.where(lane_atom == a, bd[pl.ds(a, KP, stride=4), :][:, 0:SLOT], 0.0)
        dsend[h, 0:KP, 0:SLOT] = packed
    remote(dsend.at[1 - c], drecv.at[7], dens_r.at[7], at(dc=1))
    arrived(drecv.at[7], dens_r.at[7])
    dpart[...] = dsend[c] + drecv[7]
    for dz in range(2):
        for dx in range(4):
            if dz or dx:
                j = dz * 4 + (4 - dx) % 4 - 1
                remote(dpart, drecv.at[j], dens_r.at[j], at(dz=dz, dx=dx))
    for j in range(7):
        arrived(drecv.at[j], dens_r.at[j])
    density = dpart[...]
    for j in range(7):
        density = density + drecv[j]
    density = density * (1.0 / bands_all)

    lane = lax.broadcasted_iota(jnp.int32, (K, SLOT), 1)
    grad_t = jnp.zeros((K, SLOT), F32)
    slot = 2 * ga + c
    for a in range(4):
        kind = species_ref[4 * slot + a]
        acc = jnp.zeros((K, HID), F32)
        for k in range(K):
            acc = acc + density[0:K, 4 * k + a:4 * k + a + 1] * lin[kind, k * K:(k + 1) * K, :]
        preact = jnp.sum(acc, axis=0, keepdims=True) + bias_ref[kind]
        act = jnp.tanh(preact)
        slope = lout_ref[kind] * (1.0 - act * act)
        for k in range(K):
            column = jnp.sum(lin[kind, k * K:(k + 1) * K, :] * slope, axis=1, keepdims=True)
            grad_t = jnp.where(lane == 4 * k + a, column, grad_t)
    bd[...] = jnp.zeros((SLOT, 128), F32)
    pad = jnp.zeros((K, 128 - SLOT), F32)
    for a in range(4):
        bd[pl.ds(a, K, stride=4), :] = jnp.concatenate([jnp.where(lane % 4 == a, grad_t, 0.0), pad], axis=1)
    square = bd[:, 0:SLOT]
    bd[:, 0:SLOT] = square + square.T
    packed = jnp.zeros((KP, 128), F32)
    for a in range(4):
        packed = packed + bd[pl.ds(a, KP, stride=4), :]
    xs[0:KP, :] = packed
    xall[slot] = xs[...]
    for dy in range(4):
        for dl in range(2):
            for dc in range(2):
                if dy or dl or dc:
                    j = (((4 - dy) % 4) * 2 + dl) * 2 + dc
                    remote(xs, xall.at[slot], xsr.at[j], at(dy=dy, dl=dl, dc=dc))
    for dy in range(4):
        for dl in range(2):
            for dc in range(2):
                if dy or dl or dc:
                    j = (dy * 2 + dl) * 2 + dc
                    from_slot = 2 * (((y + dy) % 4) * 2 + (zl + dl) % 2) + (c + dc) % 2
                    arrived(xall.at[from_slot], xsr.at[j])

    factor = 1.0 / math.sqrt(64 * K)
    rows4 = lax.broadcasted_iota(jnp.int32, (SLOT, SLOT), 0) % 4
    lanes4 = lax.broadcasted_iota(jnp.int32, (SLOT, SLOT), 1) % 4
    same = rows4 == lanes4

    def apply(pair, carry):
        for h in range(2):
            j = 2 * pair + h
            for a in range(4):
                bds[j, pl.ds(a, KP, stride=4), :] = xall[j, 0:KP, :]
            full = jnp.where(same, bds[j, :, 0:SLOT], 0.0)
            high = full.astype(BF16)
            low = (full - high.astype(F32)).astype(BF16)
            coef = coef_of(pair, h)
            got = jnp.dot(high, coef, preferred_element_type=F32) + jnp.dot(low, coef, preferred_element_type=F32)
            appt[pl.ds(pl.multiple_of(j * SLOT, 16), SLOT), :] = (got * factor).astype(BF16)
        return carry

    lax.fori_loop(0, 8, apply, 0, unroll=2)

    def turn(j, carry):
        block = pl.ds(pl.multiple_of(j * 256, 256), 256)
        app[:, block] = appt[block, :].T
        return carry

    lax.fori_loop(0, 7, turn, 0)
    for copy in sends[-POOL:]:
        copy.wait_send()


def correct_kernel(app, tab, out_hbm, out, sems):
    def store(t):
        cols = pl.ds(pl.multiple_of(t * 512, 512), 512)
        return pltpu.make_async_copy(out.at[:, cols], out_hbm.at[:, cols], sems.at[t])

    def one(t, carry):
        cols = pl.ds(pl.multiple_of(t * 512, 512), 512)
        out[:, cols] = jnp.dot(app[...], tab[:, cols], preferred_element_type=F32).astype(BF16)
        store(t).start()
        return carry

    steps = out.shape[1] // 512
    lax.fori_loop(0, steps, one, 0)
    for t in range(steps):
        store(t).wait()


def body(wave_coef, projector, occupation, species, layer_in, bias_in, layer_out):
    atoms_here, orbitals, gs = projector.shape
    bands = wave_coef.shape[0]
    bands_all = bands * lax.axis_size("band")
    assert atoms_here == 4 and orbitals == K and bands == 512
    hbm = pl.BlockSpec(memory_space=pltpu.HBM)
    vmem = pl.BlockSpec(memory_space=pltpu.VMEM)
    smem = pl.BlockSpec(memory_space=pltpu.SMEM)
    dma = pltpu.SemaphoreType.DMA
    applied, table = pl.pallas_call(
        functools.partial(body_kernel, bands_all),
        out_shape=[pltpu.VMEM((bands, 16 * SLOT), BF16), pltpu.VMEM((16 * SLOT, gs), BF16)],
        in_specs=[hbm, hbm, vmem, smem, hbm, vmem, vmem],
        out_specs=[vmem, vmem],
        scratch_shapes=[
            pltpu.VMEM((bands, gs), BF16),
            pltpu.VMEM((K, 4, gs), BF16),
            pltpu.VMEM((HID, SPECIES, K * K), F32),
            pltpu.VMEM((8, PAIR, bands), F32),
            pltpu.VMEM((8, PAIR, bands), BF16),
            pltpu.VMEM((8, 3, PAIR, 128), BF16),
            pltpu.VMEM((8, PAIR, 128), BF16),
            pltpu.VMEM((8, PAIR, 128), BF16),
            pltpu.VMEM((16 * SLOT, bands), BF16),
            pltpu.VMEM((SPECIES, K * K, HID), F32),
            pltpu.VMEM((2, 32, 128), F32),
            pltpu.VMEM((32, 128), F32),
            pltpu.VMEM((8, 32, 128), F32),
            pltpu.VMEM((32, 128), F32),
            pltpu.VMEM((16, 32, 128), F32),
            pltpu.VMEM((16 * SLOT, bands), BF16),
            pltpu.VMEM((SLOT, 128), F32),
            pltpu.VMEM((16, SLOT, 128), F32),
            dma((3,)), dma((POOL,)), dma((NT,)), dma((16,)), dma((NP,)), dma((NP,)), dma((NP, 3)), dma((8,)), dma((16,)),
        ],
        compiler_params=pltpu.CompilerParams(
            collective_id=0, has_side_effects=True, vmem_limit_bytes=44 * 2**20
        ),
        name="step",
    )(wave_coef, jnp.transpose(projector, (1, 0, 2)), occupation.reshape(1, bands), species,
      jnp.transpose(layer_in, (2, 0, 1)), bias_in.reshape(-1, 1, HID), layer_out.reshape(-1, 1, HID))
    return pl.pallas_call(
        correct_kernel,
        out_shape=jax.ShapeDtypeStruct((bands, gs), BF16),
        in_specs=[vmem, vmem],
        out_specs=pl.BlockSpec(memory_space=pl.ANY),
        scratch_shapes=[pltpu.VMEM((bands, gs), BF16), dma((gs // 512,))],
        compiler_params=pltpu.CompilerParams(vmem_limit_bytes=16 * 2**20),
        name="correct",
    )(applied, table)


def solution(mesh):
    in_specs = (P("band", "ga"), P("band", None, "ga"), P("band"), P(), P(), P(), P())
    out_specs = P("band", "ga")
    return jax.shard_map(body, mesh=mesh, in_specs=in_specs, out_specs=out_specs, check_vma=False)
```

time: 109 us -> 107 us (0.982)
  local copies, waits for them, and re-layouts: 2.02 us -> 0 us
    unnamed x1 -> x0, local copies, waits for them, and re-layouts: 2.02 us -> none
    pallas_call x1 -> x2, Pallas kernels: 107 us -> 107 us  [the longest x1 96.9 us: body(): pl.pallas_call(functools.partial(body_kernel, bands_all), out_shape=[pltp...]
where the time goes in v5:
time: 107 us
  Pallas kernels  107 us (100%)
    pallas_call x1, Pallas kernels, body(): pl.pallas_call(functools.partial(body_kernel, bands_all), out_shape=[pltp...  96.9 us
    pallas_call x1, Pallas kernels, body(): pl.pallas_call(correct_kernel, out_shape=jax.ShapeDtypeStruct((bands, gs)...  9.85 us

profile of v5, /device:TPU:1, one launch (start us, length us, event | category | flops | bytes accessed | tf_op | source)
XLA Modules:
  0.0 106.7 jit_solution(4749094232621240813)
XLA Ops:
  0.0 96.9 %step.1 = (bf16[512,1792]{1,0:T(8,128)(2,1)S(1)}, bf16[1792,4096]{1,0:T(8,128)(2,1)S(1)}) custom-call(bf16[512,4096]{1,0:T(8,128)(2,1)} %w_hbm.1, bf16[27,4,4096]{2,1,0:T(4,128)(2,1)} %bitcast.6, f32[1,512]{1,0:T(1,128)} %bitcast.7, s32[64]{0:T(128)} %species_ref.1, f32[100,4,729]{2,1,0:T(4,128)} %bitcast.5, f32[4,1,100]{2,1,0:T(1,128)} %bitcast.8, ...), custom_call_target="tpu_custom_call" | custom-call | tf_op jit(solution)/shard_map/step/pallas_call | solution.py:492
  96.9 9.9 %correct.1 = bf16[512,4096]{1,0:T(8,128)(2,1)} custom-call(bf16[512,1792]{1,0:T(8,128)(2,1)S(1)} %get-tuple-element.7.app, bf16[1792,4096]{1,0:T(8,128)(2,1)S(1)} %get-tuple-element.8.tab), custom_call_target="tpu_custom_call" | custom-call | tf_op jit(solution)/shard_map/correct/pallas_call | solution.py:524

commit v6 on v5

--- a/solution.py
+++ b/solution.py
@@ -21,17 +21,18 @@
 
 ORDER = ((0, 0), (0, 3), (0, 1), (1, 0), (1, 3), (1, 1), (0, 2), (1, 2))
 
-SPLIT = (1, 2, 4, 5, 7)
-TABLE_ROWS = ((0, 80), (144, 80), (80, 64))
+SPANS = ((0, 32), (192, 32), (32, 48), (144, 48), (80, 64))
+CUTS = {0: "E", 3: "E", 6: "XL", 7: "XEL"}
+SIZES = {"E": (224,), "EL": (160, 64), "XL": (64, 160), "XEL": (64, 96, 64)}
 PIECES = []
-EARLY, LATE = {}, {}
+PART = {}
 for _i in range(8):
-    EARLY[_i] = len(PIECES)
-    if _i in SPLIT:
-        LATE[_i] = EARLY[_i] + 1
-        PIECES += [(_i, 0, 160), (_i, 160, 64)]
-    else:
-        PIECES += [(_i, 0, PAIR)]
+    _cut = CUTS.get(_i, "EL")
+    _row = 0
+    for _name, _size in zip(_cut, SIZES[_cut]):
+        PART[str(_i) + _name] = len(PIECES)
+        PIECES.append((_i, _row, _size))
+        _row += _size
 NP = len(PIECES)
 POOL = 64
 
@@ -48,7 +49,7 @@
 
 
 def body_kernel(bands_all, w_hbm, p_hbm, occ_ref, species_ref, lin_hbm, bias_ref, lout_ref, app, tab,
-                w, pin, lraw, part, part16, ry, zs, zr, cfull, lin, dsend, dpart, drecv, xs, xall, appt, bd, bds,
+                w, wt, pin, lraw, part, part16, ry, zs, zr, cfull, lin, dsend, dpart, drecv, xs, xall, appt, bd, bds,
                 lsem, pool, tsr, d2r, ryr, zsr, agr, dens_r, xsr):
     band = lax.axis_index("band")
     ga = lax.axis_index("ga")
@@ -134,9 +135,11 @@
         _, first, count = TREE[i]
         arrived(rows(tab, slot_row(dz, dx, 0) + row_in_slot(first, count), count), tsr.at[i])
 
+    crossings = {}
+
     def crossing(i, part):
-        first, count = ((0, SLOT), (0, 80), (80, 32))[part]
-        return ORDER[i], first, count, i + 8 * (part == 2)
+        first, count = ((0, SLOT), (0, 80), (80, 32), (0, 32), (32, 80), (32, 48))[part]
+        return ORDER[i], first, count, crossings.setdefault((i, part), len(crossings))
 
     def across(i, part=0):
         (dz, dx), first, count, sem = crossing(i, part)
@@ -160,22 +163,31 @@
             cols = pl.ds(pl.multiple_of(t * 256, 256), 256)
 
             def times(table):
-                return lax.dot_general(table, w[cols, :], (((1,), (1,)), ((), ())), preferred_element_type=F32)
+                if i == 0:
+                    dims, by = (((1,), (1,)), ((), ())), w[cols, :]
+                else:
+                    dims, by = (((1,), (0,)), ((), ())), wt[:, cols]
+                return lax.dot_general(table, by, dims, preferred_element_type=F32)
 
             def keep(to, got):
                 part[i, to:to + got.shape[0], cols] = got
                 part16[i, to:to + got.shape[0], cols] = got.astype(BF16)
 
+            spans = []
+            to = 0
+            for span in SPANS:
+                if first <= to < first + count:
+                    spans.append(span)
+                to += span[1]
             if count == PAIR:
                 got = times(read(0, PAIR))
                 to = 0
-                for start, size in TABLE_ROWS:
+                for start, size in spans:
                     keep(to, got[start:start + size])
                     to += size
-            elif first == 0:
-                keep(0, times(jnp.concatenate([read(*span) for span in TABLE_ROWS[:2]], axis=0)))
             else:
-                keep(first, times(read(*TABLE_ROWS[2])))
+                table = [read(*span) for span in spans]
+                keep(first, times(table[0] if len(table) == 1 else jnp.concatenate(table, axis=0)))
             return carry
 
         lax.fori_loop(0, 2, half, 0)
@@ -227,31 +239,40 @@
             arrived(block(s, dy), agr.at[s, dy - 1])
 
     def coef_of(pair, h):
-        cuts = ((0, 80), (160, 32)) if h == 0 else ((192, 32), (80, 80))
+        cuts = ((0, 32), (64, 48), (160, 32)) if h == 0 else ((192, 32), (112, 48), (32, 32))
         return jnp.concatenate([cfull[pl.ds(pl.multiple_of(pair * PAIR + a, 16), n), :] for a, n in cuts], axis=0)
 
     tree_send("z10", 0, 0, over)
     tree_send("x03", 0, 0, right)
     tree_send("x01", 0, 0, left)
-    across(0)
+    across(0, 0)
     tree_send("z03a", 0, 0, right)
     tree_send("z01a", 0, 0, left)
     tree_send("z03b", 0, 0, right)
     tree_send("z01b", 0, 0, left)
     wcopy.wait()
-    across_wait(0)
-    project(EARLY[0])
+    across_wait(0, 0)
+    project(PART["0E"])
     tree_wait("x03", 0, 3)
     tree_send("x02a", 0, 3, right)
     tree_wait("x01", 0, 1)
     tree_send("x02b", 0, 1, left)
-    reduce_y(EARLY[0])
+    reduce_y(PART["0E"])
     tree_send("x10", 0, 0, over)
     tree_send("x13", 0, 3, over)
     tree_send("x11", 0, 1, over)
+
+    def turn_wave(t, carry):
+        block = pl.ds(pl.multiple_of(t * 256, 256), 256)
+        wt[block, :] = w[:, block].T
+        return carry
+
+    lax.fori_loop(0, w.shape[1] // 256, turn_wave, 0)
     lcopy.wait()
     for kind in range(SPECIES):
-        lin[kind] = lraw[:, kind, :].T
+        turned = lraw[:, kind, :].T
+        for k in range(K):
+            lin[kind, k, 0:K, :] = turned[k * K:(k + 1) * K, :]
     tree_wait("z03a", 0, 3)
     across(1, 1)
     tree_wait("z01a", 0, 1)
@@ -262,33 +283,36 @@
     tree_send("z13b", 1, 0, right)
     tree_send("z11b", 1, 0, left)
     tree_send("z02a", 0, 3, right)
-    reduce_z(EARLY[0])
+    reduce_z(PART["0E"])
     across_wait(1, 1)
-    project(EARLY[1])
+    project(PART["1E"])
     across_wait(2, 1)
-    project(EARLY[2])
+    project(PART["2E"])
     tree_wait("z03b", 0, 3)
     across(1, 2)
     tree_wait("z01b", 0, 1)
     tree_send("z02b", 0, 1, left)
     across(2, 2)
     tree_wait("x10", 1, 0)
-    across(3)
+    across(3, 0)
     across_wait(1, 2)
-    project(LATE[1])
-    relay(EARLY[0])
-    reduce_y(EARLY[1])
+    project(PART["1L"])
+    relay(PART["0E"])
+    reduce_y(PART["1E"])
     across_wait(2, 2)
-    project(LATE[2])
-    reduce_y(EARLY[2])
-    across_wait(3)
-    project(EARLY[3])
-    reduce_y(LATE[1])
-    reduce_y(LATE[2])
+    project(PART["2L"])
+    reduce_y(PART["2E"])
+    across_wait(3, 0)
+    project(PART["3E"])
     tree_wait("x02a", 0, 2)
     tree_wait("x02b", 0, 2)
+    across(6, 3)
+    reduce_y(PART["1L"])
+    reduce_y(PART["2L"])
     tree_send("x12a", 0, 2, over)
     tree_send("x12b", 0, 2, over)
+    across_wait(6, 3)
+    project(PART["6X"])
     tree_wait("z13a", 1, 3)
     tree_send("z12a", 1, 3, right)
     tree_wait("z11a", 1, 1)
@@ -297,69 +321,75 @@
     across(4, 1)
     tree_wait("x11", 1, 1)
     across(5, 1)
-    reduce_y(EARLY[3])
+    reduce_y(PART["3E"])
     across_wait(4, 1)
-    project(EARLY[4])
+    project(PART["4E"])
     across_wait(5, 1)
-    project(EARLY[5])
-    reduce_z(EARLY[1])
-    reduce_z(EARLY[2])
+    project(PART["5E"])
+    reduce_z(PART["1E"])
+    reduce_z(PART["2E"])
     tree_wait("z13b", 1, 3)
     tree_send("z12c", 1, 3, right)
     across(4, 2)
     tree_wait("z11b", 1, 1)
     tree_send("z12d", 1, 1, left)
     across(5, 2)
-    reduce_z(LATE[1])
-    reduce_z(LATE[2])
+    reduce_z(PART["1L"])
+    reduce_z(PART["2L"])
+    reduce_y(PART["6X"])
     across_wait(4, 2)
-    project(LATE[4])
-    reduce_y(EARLY[4])
+    project(PART["4L"])
+    reduce_y(PART["4E"])
     across_wait(5, 2)
-    project(LATE[5])
-    reduce_y(EARLY[5])
-    reduce_z(EARLY[3])
-    relay(EARLY[1])
-    relay(EARLY[2])
-    tree_wait("z02a", 0, 2)
-    across(6, 1)
-    tree_wait("z02b", 0, 2)
-    across(6, 2)
-    reduce_y(LATE[4])
-    reduce_y(LATE[5])
-    relay(LATE[1])
-    relay(LATE[2])
-    reduce_z(EARLY[4])
-    across_wait(6, 1)
-    across_wait(6, 2)
-    project(EARLY[6])
-    reduce_z(EARLY[5])
-    relay(EARLY[3])
+    project(PART["5L"])
+    reduce_z(PART["3E"])
+    reduce_z(PART["6X"])
+    relay(PART["1E"])
+    relay(PART["2E"])
     tree_wait("x12a", 1, 2)
     tree_wait("x12b", 1, 2)
+    across(7, 3)
+    reduce_y(PART["5E"])
+    reduce_z(PART["4E"])
+    tree_wait("z02a", 0, 2)
+    tree_wait("z02b", 0, 2)
+    across(6, 4)
+    across_wait(7, 3)
+    project(PART["7X"])
+    reduce_y(PART["4L"])
+    reduce_y(PART["5L"])
+    relay(PART["1L"])
+    relay(PART["2L"])
+    reduce_z(PART["5E"])
+    across_wait(6, 4)
+    project(PART["6L"])
     tree_wait("z12a", 1, 2)
     tree_wait("z12b", 1, 2)
-    across(7, 1)
-    reduce_z(LATE[4])
-    reduce_z(LATE[5])
-    across_wait(7, 1)
-    project(EARLY[7])
+    across(7, 5)
+    reduce_z(PART["4L"])
+    reduce_z(PART["5L"])
+    across_wait(7, 5)
+    project(PART["7E"])
+    relay(PART["3E"])
+    relay(PART["6X"])
+    reduce_y(PART["7X"])
     tree_wait("z12c", 1, 2)
     tree_wait("z12d", 1, 2)
     across(7, 2)
+    relay(PART["4E"])
+    relay(PART["5E"])
     across_wait(7, 2)
-    project(LATE[7])
-    reduce_y(EARLY[6])
-    relay(EARLY[4])
-    relay(EARLY[5])
-    reduce_y(EARLY[7])
-    reduce_y(LATE[7])
-    relay(LATE[4])
-    relay(LATE[5])
-    reduce_z(EARLY[6])
-    reduce_z(EARLY[7])
-    reduce_z(LATE[7])
-    relay(EARLY[6])
+    project(PART["7L"])
+    reduce_y(PART["6L"])
+    reduce_z(PART["7X"])
+    reduce_y(PART["7E"])
+    reduce_y(PART["7L"])
+    reduce_z(PART["6L"])
+    reduce_z(PART["7E"])
+    reduce_z(PART["7L"])
+    relay(PART["4L"])
+    relay(PART["5L"])
+    relay(PART["6L"])
     for s in range(NP):
         gathered(s)
 
@@ -401,12 +431,12 @@
         kind = species_ref[4 * slot + a]
         acc = jnp.zeros((K, HID), F32)
         for k in range(K):
-            acc = acc + density[0:K, 4 * k + a:4 * k + a + 1] * lin[kind, k * K:(k + 1) * K, :]
+            acc = acc + density[0:K, 4 * k + a:4 * k + a + 1] * lin[kind, k, 0:K, :]
         preact = jnp.sum(acc, axis=0, keepdims=True) + bias_ref[kind]
         act = jnp.tanh(preact)
         slope = lout_ref[kind] * (1.0 - act * act)
         for k in range(K):
-            column = jnp.sum(lin[kind, k * K:(k + 1) * K, :] * slope, axis=1, keepdims=True)
+            column = jnp.sum(lin[kind, k, 0:K, :] * slope, axis=1, keepdims=True)
             grad_t = jnp.where(lane == 4 * k + a, column, grad_t)
     bd[...] = jnp.zeros((SLOT, 128), F32)
     pad = jnp.zeros((K, 128 - SLOT), F32)
@@ -465,16 +495,16 @@
 
 def correct_kernel(app, tab, out_hbm, out, sems):
     def store(t):
-        cols = pl.ds(pl.multiple_of(t * 512, 512), 512)
+        cols = pl.ds(pl.multiple_of(t * 1024, 1024), 1024)
         return pltpu.make_async_copy(out.at[:, cols], out_hbm.at[:, cols], sems.at[t])
 
     def one(t, carry):
-        cols = pl.ds(pl.multiple_of(t * 512, 512), 512)
+        cols = pl.ds(pl.multiple_of(t * 1024, 1024), 1024)
         out[:, cols] = jnp.dot(app[...], tab[:, cols], preferred_element_type=F32).astype(BF16)
         store(t).start()
         return carry
 
-    steps = out.shape[1] // 512
+    steps = out.shape[1] // 1024
     lax.fori_loop(0, steps, one, 0)
     for t in range(steps):
         store(t).wait()
@@ -496,6 +526,7 @@
         out_specs=[vmem, vmem],
         scratch_shapes=[
             pltpu.VMEM((bands, gs), BF16),
+            pltpu.VMEM((gs, bands), BF16),
             pltpu.VMEM((K, 4, gs), BF16),
             pltpu.VMEM((HID, SPECIES, K * K), F32),
             pltpu.VMEM((8, PAIR, bands), F32),
@@ -504,7 +535,7 @@
             pltpu.VMEM((8, PAIR, 128), BF16),
             pltpu.VMEM((8, PAIR, 128), BF16),
             pltpu.VMEM((16 * SLOT, bands), BF16),
-            pltpu.VMEM((SPECIES, K * K, HID), F32),
+            pltpu.VMEM((SPECIES, K, 32, HID), F32),
             pltpu.VMEM((2, 32, 128), F32),
             pltpu.VMEM((32, 128), F32),
             pltpu.VMEM((8, 32, 128), F32),
@@ -526,7 +557,7 @@
         out_shape=jax.ShapeDtypeStruct((bands, gs), BF16),
         in_specs=[vmem, vmem],
         out_specs=pl.BlockSpec(memory_space=pl.ANY),
-        scratch_shapes=[pltpu.VMEM((bands, gs), BF16), dma((gs // 512,))],
+        scratch_shapes=[pltpu.VMEM((bands, gs), BF16), dma((gs // 1024,))],
         compiler_params=pltpu.CompilerParams(vmem_limit_bytes=16 * 2**20),
         name="correct",
     )(applied, table)

time: 107 us -> 102 us (0.953)
  Pallas kernels: 107 us -> 102 us
    pallas_call x1, Pallas kernels: 96.9 us -> 92.9 us  [body(): pl.pallas_call(functools.partial(body_kernel, bands_all), out_shape=[pltp...]
where the time goes in v6:
time: 102 us
  Pallas kernels  102 us (100%)
    pallas_call x1, Pallas kernels, body(): pl.pallas_call(functools.partial(body_kernel, bands_all), out_shape=[pltp...  92.9 us
    pallas_call x1, Pallas kernels, body(): pl.pallas_call(correct_kernel, out_shape=jax.ShapeDtypeStruct((bands, gs)...  9.26 us

profile of v6, /device:TPU:1, one launch (start us, length us, event | category | flops | bytes accessed | tf_op | source)
XLA Modules:
  0.0 102.2 jit_solution(10381111597174301011)
XLA Ops:
  0.0 92.9 %step.1 = (bf16[512,1792]{1,0:T(8,128)(2,1)S(1)}, bf16[1792,4096]{1,0:T(8,128)(2,1)S(1)}) custom-call(bf16[512,4096]{1,0:T(8,128)(2,1)} %w_hbm.1, bf16[27,4,4096]{2,1,0:T(4,128)(2,1)} %bitcast.6, f32[1,512]{1,0:T(1,128)} %bitcast.7, s32[64]{0:T(128)} %species_ref.1, f32[100,4,729]{2,1,0:T(4,128)} %bitcast.5, f32[4,1,100]{2,1,0:T(1,128)} %bitcast.8, ...), custom_call_target="tpu_custom_call" | custom-call | tf_op jit(solution)/shard_map/step/pallas_call | solution.py:522
  93.0 9.3 %correct.1 = bf16[512,4096]{1,0:T(8,128)(2,1)} custom-call(bf16[512,1792]{1,0:T(8,128)(2,1)S(1)} %get-tuple-element.7.app, bf16[1792,4096]{1,0:T(8,128)(2,1)S(1)} %get-tuple-element.8.tab), custom_call_target="tpu_custom_call" | custom-call | tf_op jit(solution)/shard_map/correct/pallas_call | solution.py:555

commit v7 on v6

--- a/solution.py
+++ b/solution.py
@@ -34,7 +34,7 @@
         PIECES.append((_i, _row, _size))
         _row += _size
 NP = len(PIECES)
-POOL = 64
+POOL = 40
 
 TREE = (
     ("z10", 32, 80), ("x10", 0, 32),
@@ -50,7 +50,7 @@
 
 def body_kernel(bands_all, w_hbm, p_hbm, occ_ref, species_ref, lin_hbm, bias_ref, lout_ref, app, tab,
                 w, wt, pin, lraw, part, part16, ry, zs, zr, cfull, lin, dsend, dpart, drecv, xs, xall, appt, bd, bds,
-                lsem, pool, tsr, d2r, ryr, zsr, agr, dens_r, xsr):
+                lsem, pool, tss, tsr, d2r, ryr, zsr, agr, dens_r, xsr, rounds):
     band = lax.axis_index("band")
     ga = lax.axis_index("ga")
     zh, x, c = band // 8, (band // 2) % 4, band % 2
@@ -83,17 +83,8 @@
     lcopy.start()
 
     barrier = pltpu.get_barrier_semaphore()
-    partners = [at(dc=1)]
-    for dz in range(2):
-        for dx in range(4):
-            if dz or dx:
-                partners.append(at(dz=dz, dx=dx))
-    for dy in range(4):
-        for dl in range(2):
-            if dy or dl:
-                partners.append(at(dy=dy, dl=dl))
-                partners.append(at(dy=dy, dl=dl, dc=1))
-    for partner in partners:
+    near = [at(dc=1), at(dx=1), at(dx=3), at(dz=1), at(dy=1), at(dy=3), at(dl=1)]
+    for partner in near:
         pl.semaphore_signal(barrier, inc=1, device_id=partner, device_id_type=MESH)
     pcopy.wait()
 
@@ -105,19 +96,36 @@
         return carry
 
     lax.fori_loop(0, 8, pack, 0)
-    pl.semaphore_wait(barrier, len(partners))
+    pl.semaphore_wait(barrier, len(near))
+
+    def tell(r):
+        for partner in near:
+            pl.semaphore_signal(rounds.at[r], inc=1, device_id=partner, device_id_type=MESH)
+
+    def known(r):
+        pl.semaphore_wait(rounds.at[r], len(near))
+        if r < 2:
+            tell(r + 1)
+
 
     sends = []
 
-    def remote(src, dst, rs, device):
-        n = len(sends)
-        if n >= POOL:
-            sends[n - POOL].wait_send()
+    pooled = []
+
+    def remote(src, dst, rs, device, own=None):
+        n = len(pooled)
+        if own is None:
+            if n >= POOL:
+                pooled[n - POOL].wait_send()
+            own = pool.at[n % POOL]
+            keep = pooled
+        else:
+            keep = sends
         copy = pltpu.make_async_remote_copy(
-            src_ref=src, dst_ref=dst, send_sem=pool.at[n % POOL], recv_sem=rs, device_id=device, device_id_type=MESH
+            src_ref=src, dst_ref=dst, send_sem=own, recv_sem=rs, device_id=device, device_id_type=MESH
         )
         copy.start()
-        sends.append(copy)
+        keep.append(copy)
 
     def arrived(dst, rs):
         pltpu.make_async_remote_copy(
@@ -128,7 +136,7 @@
         i = TREE_ID[name]
         _, first, count = TREE[i]
         ref = rows(tab, slot_row(dz, dx, 0) + row_in_slot(first, count), count)
-        remote(ref, ref, tsr.at[i], device)
+        remote(ref, ref, tsr.at[i], device, tss.at[i])
 
     def tree_wait(name, dz, dx):
         i = TREE_ID[name]
@@ -242,6 +250,7 @@
         cuts = ((0, 32), (64, 48), (160, 32)) if h == 0 else ((192, 32), (112, 48), (32, 32))
         return jnp.concatenate([cfull[pl.ds(pl.multiple_of(pair * PAIR + a, 16), n), :] for a, n in cuts], axis=0)
 
+    tell(0)
     tree_send("z10", 0, 0, over)
     tree_send("x03", 0, 0, right)
     tree_send("x01", 0, 0, left)
@@ -251,6 +260,7 @@
     tree_send("z03b", 0, 0, right)
     tree_send("z01b", 0, 0, left)
     wcopy.wait()
+    known(0)
     across_wait(0, 0)
     project(PART["0E"])
     tree_wait("x03", 0, 3)
@@ -258,6 +268,7 @@
     tree_wait("x01", 0, 1)
     tree_send("x02b", 0, 1, left)
     reduce_y(PART["0E"])
+    known(1)
     tree_send("x10", 0, 0, over)
     tree_send("x13", 0, 3, over)
     tree_send("x11", 0, 1, over)
@@ -298,6 +309,7 @@
     across_wait(1, 2)
     project(PART["1L"])
     relay(PART["0E"])
+    known(2)
     reduce_y(PART["1E"])
     across_wait(2, 2)
     project(PART["2L"])
@@ -370,12 +382,12 @@
     reduce_z(PART["5L"])
     across_wait(7, 5)
     project(PART["7E"])
+    tree_wait("z12c", 1, 2)
+    tree_wait("z12d", 1, 2)
+    across(7, 2)
     relay(PART["3E"])
     relay(PART["6X"])
     reduce_y(PART["7X"])
-    tree_wait("z12c", 1, 2)
-    tree_wait("z12d", 1, 2)
-    across(7, 2)
     relay(PART["4E"])
     relay(PART["5E"])
     across_wait(7, 2)
@@ -409,16 +421,15 @@
         for a in range(4):
             packed = packed + jnp.where(lane_atom == a, bd[pl.ds(a, KP, stride=4), :][:, 0:SLOT], 0.0)
         dsend[h, 0:KP, 0:SLOT] = packed
-    remote(dsend.at[1 - c], drecv.at[7], dens_r.at[7], at(dc=1))
-    arrived(drecv.at[7], dens_r.at[7])
+    remote(dsend.at[1 - c], drecv.at[7], dens_r.at[1], at(dc=1))
+    arrived(drecv.at[7], dens_r.at[1])
     dpart[...] = dsend[c] + drecv[7]
     for dz in range(2):
         for dx in range(4):
             if dz or dx:
                 j = dz * 4 + (4 - dx) % 4 - 1
-                remote(dpart, drecv.at[j], dens_r.at[j], at(dz=dz, dx=dx))
-    for j in range(7):
-        arrived(drecv.at[j], dens_r.at[j])
+                remote(dpart, drecv.at[j], dens_r.at[0], at(dz=dz, dx=dx))
+    arrived(drecv.at[pl.ds(0, 7)], dens_r.at[0])
     density = dpart[...]
     for j in range(7):
         density = density + drecv[j]
@@ -489,7 +500,7 @@
         return carry
 
     lax.fori_loop(0, 7, turn, 0)
-    for copy in sends[-POOL:]:
+    for copy in sends + pooled[-POOL:]:
         copy.wait_send()
 
 
@@ -544,7 +555,7 @@
             pltpu.VMEM((16 * SLOT, bands), BF16),
             pltpu.VMEM((SLOT, 128), F32),
             pltpu.VMEM((16, SLOT, 128), F32),
-            dma((3,)), dma((POOL,)), dma((NT,)), dma((16,)), dma((NP,)), dma((NP,)), dma((NP, 3)), dma((8,)), dma((16,)),
+            dma((3,)), dma((POOL,)), dma((NT,)), dma((NT,)), dma((16,)), dma((NP,)), dma((NP,)), dma((NP, 3)), dma((2,)), dma((16,)), pltpu.SemaphoreType.REGULAR((3,)),
         ],
         compiler_params=pltpu.CompilerParams(
             collective_id=0, has_side_effects=True, vmem_limit_bytes=44 * 2**20

time: 102 us -> 102 us (level)
  no operation moved by 1% of the time
where the time goes in v7:
time: 102 us
  Pallas kernels  102 us (100%)
    pallas_call x1, Pallas kernels, body(): pl.pallas_call(functools.partial(body_kernel, bands_all), out_shape=[pltp...  92.2 us
    pallas_call x1, Pallas kernels, body(): pl.pallas_call(correct_kernel, out_shape=jax.ShapeDtypeStruct((bands, gs)...  9.26 us

profile of v7, /device:TPU:1, one launch (start us, length us, event | category | flops | bytes accessed | tf_op | source)
XLA Modules:
  0.0 101.5 jit_solution(16619588081125914474)
XLA Ops:
  0.0 92.2 %step.1 = (bf16[512,1792]{1,0:T(8,128)(2,1)S(1)}, bf16[1792,4096]{1,0:T(8,128)(2,1)S(1)}) custom-call(bf16[512,4096]{1,0:T(8,128)(2,1)} %w_hbm.1, bf16[27,4,4096]{2,1,0:T(4,128)(2,1)} %bitcast.6, f32[1,512]{1,0:T(1,128)} %bitcast.7, s32[64]{0:T(128)} %species_ref.1, f32[100,4,729]{2,1,0:T(4,128)} %bitcast.5, f32[4,1,100]{2,1,0:T(1,128)} %bitcast.8, ...), custom_call_target="tpu_custom_call" | custom-call | tf_op jit(solution)/shard_map/step/pallas_call | solution.py:533
  92.3 9.3 %correct.1 = bf16[512,4096]{1,0:T(8,128)(2,1)} custom-call(bf16[512,1792]{1,0:T(8,128)(2,1)S(1)} %get-tuple-element.7.app, bf16[1792,4096]{1,0:T(8,128)(2,1)S(1)} %get-tuple-element.8.tab), custom_call_target="tpu_custom_call" | custom-call | tf_op jit(solution)/shard_map/correct/pallas_call | solution.py:566

commit v8 on v7

--- a/solution.py
+++ b/solution.py
@@ -416,7 +416,7 @@
         gram = lax.dot_general(high, coef, dims, preferred_element_type=F32) + lax.dot_general(
             low, coef, dims, preferred_element_type=F32
         )
-        bd[:, 0:SLOT] = gram
+        bd[0:SLOT, 0:SLOT] = gram
         packed = jnp.zeros((KP, SLOT), F32)
         for a in range(4):
             packed = packed + jnp.where(lane_atom == a, bd[pl.ds(a, KP, stride=4), :][:, 0:SLOT], 0.0)
@@ -424,11 +424,9 @@
     remote(dsend.at[1 - c], drecv.at[7], dens_r.at[1], at(dc=1))
     arrived(drecv.at[7], dens_r.at[1])
     dpart[...] = dsend[c] + drecv[7]
-    for dz in range(2):
-        for dx in range(4):
-            if dz or dx:
-                j = dz * 4 + (4 - dx) % 4 - 1
-                remote(dpart, drecv.at[j], dens_r.at[0], at(dz=dz, dx=dx))
+    for dz, dx in ((1, 2), (0, 2), (1, 1), (1, 3), (1, 0), (0, 1), (0, 3)):
+        j = dz * 4 + (4 - dx) % 4 - 1
+        remote(dpart, drecv.at[j], dens_r.at[0], at(dz=dz, dx=dx))
     arrived(drecv.at[pl.ds(0, 7)], dens_r.at[0])
     density = dpart[...]
     for j in range(7):
@@ -449,30 +447,24 @@
         for k in range(K):
             column = jnp.sum(lin[kind, k, 0:K, :] * slope, axis=1, keepdims=True)
             grad_t = jnp.where(lane == 4 * k + a, column, grad_t)
-    bd[...] = jnp.zeros((SLOT, 128), F32)
+    bd[...] = jnp.zeros(bd.shape, F32)
     pad = jnp.zeros((K, 128 - SLOT), F32)
     for a in range(4):
         bd[pl.ds(a, K, stride=4), :] = jnp.concatenate([jnp.where(lane % 4 == a, grad_t, 0.0), pad], axis=1)
-    square = bd[:, 0:SLOT]
-    bd[:, 0:SLOT] = square + square.T
+    square = bd[0:SLOT, 0:SLOT]
+    bd[0:SLOT, 0:SLOT] = square + square.T
     packed = jnp.zeros((KP, 128), F32)
     for a in range(4):
         packed = packed + bd[pl.ds(a, KP, stride=4), :]
     xs[0:KP, :] = packed
-    xall[slot] = xs[...]
-    for dy in range(4):
-        for dl in range(2):
+    xall[15] = xs[...]
+    for dy in (2, 1, 3, 0):
+        for dl in (1, 0):
             for dc in range(2):
                 if dy or dl or dc:
                     j = (((4 - dy) % 4) * 2 + dl) * 2 + dc
-                    remote(xs, xall.at[slot], xsr.at[j], at(dy=dy, dl=dl, dc=dc))
-    for dy in range(4):
-        for dl in range(2):
-            for dc in range(2):
-                if dy or dl or dc:
-                    j = (dy * 2 + dl) * 2 + dc
-                    from_slot = 2 * (((y + dy) % 4) * 2 + (zl + dl) % 2) + (c + dc) % 2
-                    arrived(xall.at[from_slot], xsr.at[j])
+                    remote(xs, xall.at[j - 1], xsr.at[0], at(dy=dy, dl=dl, dc=dc))
+    arrived(xall.at[pl.ds(0, 15)], xsr.at[0])
 
     factor = 1.0 / math.sqrt(64 * K)
     rows4 = lax.broadcasted_iota(jnp.int32, (SLOT, SLOT), 0) % 4
@@ -482,9 +474,10 @@
     def apply(pair, carry):
         for h in range(2):
             j = 2 * pair + h
+            place = (((pair // 2 - y + 4) % 4 * 2 + (pair - zl + 2) % 2) * 2 + (h - c + 2) % 2 + 15) % 16
             for a in range(4):
-                bds[j, pl.ds(a, KP, stride=4), :] = xall[j, 0:KP, :]
-            full = jnp.where(same, bds[j, :, 0:SLOT], 0.0)
+                bds[j, pl.ds(a, KP, stride=4), :] = xall[place, 0:KP, :]
+            full = jnp.where(same, bds[j, 0:SLOT, 0:SLOT], 0.0)
             high = full.astype(BF16)
             low = (full - high.astype(F32)).astype(BF16)
             coef = coef_of(pair, h)
@@ -553,9 +546,9 @@
             pltpu.VMEM((32, 128), F32),
             pltpu.VMEM((16, 32, 128), F32),
             pltpu.VMEM((16 * SLOT, bands), BF16),
-            pltpu.VMEM((SLOT, 128), F32),
-            pltpu.VMEM((16, SLOT, 128), F32),
-            dma((3,)), dma((POOL,)), dma((NT,)), dma((NT,)), dma((16,)), dma((NP,)), dma((NP,)), dma((NP, 3)), dma((2,)), dma((16,)), pltpu.SemaphoreType.REGULAR((3,)),
+            pltpu.VMEM((SLOT + 8, 128), F32),
+            pltpu.VMEM((16, SLOT + 8, 128), F32),
+            dma((3,)), dma((POOL,)), dma((NT,)), dma((NT,)), dma((16,)), dma((NP,)), dma((NP,)), dma((NP, 3)), dma((2,)), dma((1,)), pltpu.SemaphoreType.REGULAR((3,)),
         ],
         compiler_params=pltpu.CompilerParams(
             collective_id=0, has_side_effects=True, vmem_limit_bytes=44 * 2**20

time: 102 us -> 101 us (level)
  no operation moved by 1% of the time
where the time goes in v8:
time: 101 us
  Pallas kernels  101 us (100%)
    pallas_call x1, Pallas kernels, body(): pl.pallas_call(functools.partial(body_kernel, bands_all), out_shape=[pltp...  91.4 us
    pallas_call x1, Pallas kernels, body(): pl.pallas_call(correct_kernel, out_shape=jax.ShapeDtypeStruct((bands, gs)...  9.26 us

profile of v8, /device:TPU:1, one launch (start us, length us, event | category | flops | bytes accessed | tf_op | source)
XLA Modules:
  0.0 100.6 jit_solution(1583673153106747786)
XLA Ops:
  0.0 91.4 %step.1 = (bf16[512,1792]{1,0:T(8,128)(2,1)S(1)}, bf16[1792,4096]{1,0:T(8,128)(2,1)S(1)}) custom-call(bf16[512,4096]{1,0:T(8,128)(2,1)} %w_hbm.1, bf16[27,4,4096]{2,1,0:T(4,128)(2,1)} %bitcast.6, f32[1,512]{1,0:T(1,128)} %bitcast.7, s32[64]{0:T(128)} %species_ref.1, f32[100,4,729]{2,1,0:T(4,128)} %bitcast.5, f32[4,1,100]{2,1,0:T(1,128)} %bitcast.8, ...), custom_call_target="tpu_custom_call" | custom-call | tf_op jit(solution)/shard_map/step/pallas_call | solution.py:526
  91.4 9.3 %correct.1 = bf16[512,4096]{1,0:T(8,128)(2,1)} custom-call(bf16[512,1792]{1,0:T(8,128)(2,1)S(1)} %get-tuple-element.7.app, bf16[1792,4096]{1,0:T(8,128)(2,1)S(1)} %get-tuple-element.8.tab), custom_call_target="tpu_custom_call" | custom-call | tf_op jit(solution)/shard_map/correct/pallas_call | solution.py:559

commit v9 on v8

--- a/solution.py
+++ b/solution.py
@@ -395,8 +395,8 @@
     reduce_y(PART["6L"])
     reduce_z(PART["7X"])
     reduce_y(PART["7E"])
+    reduce_z(PART["6L"])
     reduce_y(PART["7L"])
-    reduce_z(PART["6L"])
     reduce_z(PART["7E"])
     reduce_z(PART["7L"])
     relay(PART["4L"])

time: 101 us -> 101 us (level)
  no operation moved by 1% of the time
where the time goes in v9:
time: 101 us
  Pallas kernels  101 us (100%)
    pallas_call x1, Pallas kernels, body(): pl.pallas_call(functools.partial(body_kernel, bands_all), out_shape=[pltp...  91.3 us
    pallas_call x1, Pallas kernels, body(): pl.pallas_call(correct_kernel, out_shape=jax.ShapeDtypeStruct((bands, gs)...  9.26 us

profile of v9, /device:TPU:1, one launch (start us, length us, event | category | flops | bytes accessed | tf_op | source)
XLA Modules:
  0.0 100.5 jit_solution(15736617847723271550)
XLA Ops:
  0.0 91.3 %step.1 = (bf16[512,1792]{1,0:T(8,128)(2,1)S(1)}, bf16[1792,4096]{1,0:T(8,128)(2,1)S(1)}) custom-call(bf16[512,4096]{1,0:T(8,128)(2,1)} %w_hbm.1, bf16[27,4,4096]{2,1,0:T(4,128)(2,1)} %bitcast.6, f32[1,512]{1,0:T(1,128)} %bitcast.7, s32[64]{0:T(128)} %species_ref.1, f32[100,4,729]{2,1,0:T(4,128)} %bitcast.5, f32[4,1,100]{2,1,0:T(1,128)} %bitcast.8, ...), custom_call_target="tpu_custom_call" | custom-call | tf_op jit(solution)/shard_map/step/pallas_call | solution.py:526
  91.3 9.3 %correct.1 = bf16[512,4096]{1,0:T(8,128)(2,1)} custom-call(bf16[512,1792]{1,0:T(8,128)(2,1)S(1)} %get-tuple-element.7.app, bf16[1792,4096]{1,0:T(8,128)(2,1)S(1)} %get-tuple-element.8.tab), custom_call_target="tpu_custom_call" | custom-call | tf_op jit(solution)/shard_map/correct/pallas_call | solution.py:559
